TPU v7x, 32 devices: a whole 2x2x4 slice. The times are simulated.
32 devices in a mesh: dp: 16 (over z, x, core), tensor: 2 (over y).
Axes of the slice: x: 2, y: 2, z: 4, core: 2. Of those that a mesh axis runs over, the one named last changes fastest.
Arguments:
- tokens: bfloat16 [63040, 384], P(('dp', 'tensor')), may hold values from -6 to 6
- query_key_value: bfloat16 [384, 3, 384], P('dp', None, 'tensor'), may hold values from -0.3125 to 0.3125
- attention_out: bfloat16 [384, 384], P('tensor', 'dp'), may hold values from -1.25 to 1.25
- first_gain: bfloat16 [384], P('dp'), may hold values from 0.099609375 to 1.8984375
- first_shift: bfloat16 [384], P('dp'), may hold values from -3 to 3
- second_gain: bfloat16 [384], P('dp'), may hold values from 0.099609375 to 1.8984375
- second_shift: bfloat16 [384], P('dp'), may hold values from -3 to 3
- expert_in: bfloat16 [8, 384, 1536], P(None, None, ('dp', 'tensor')), may hold values from -0.3125 to 0.3125
- expert_out: bfloat16 [8, 1536, 384], P(None, ('dp', 'tensor')), may hold values from -0.15625 to 0.15625
- expert_ids: int32 [63040, 2], P('dp'), may hold values from 0 to 7, all different within a row; in each aligned block of 3940 rows (0 to 3939, 3940 to 7879, ...) at most 1232 rows name the same one
- gate_weights: float32 [63040, 2], P('dp'), may hold values from 0.1 to 0.9
- cotangent: bfloat16 [63040, 384], P(('dp', 'tensor')), may hold values from -6 to 6
Outputs:
- output: bfloat16 [63040, 384], P(('dp', 'tensor'))
- grad_tokens: float32 [63040, 384], P(('dp', 'tensor'))
- grad_query_key_value: float32 [384, 3, 384], P('dp', None, 'tensor')
- grad_attention_out: float32 [384, 384], P('tensor', 'dp')
- grad_first_gain: float32 [384], P('dp')
- grad_first_shift: float32 [384], P('dp')
- grad_second_gain: float32 [384], P('dp')
- grad_second_shift: float32 [384], P('dp')
- grad_expert_in: float32 [8, 384, 1536], P(None, None, ('dp', 'tensor'))
- grad_expert_out: float32 [8, 1536, 384], P(None, ('dp', 'tensor'))
Inputs may be any that keep to these rules, and one draw needn't show every extreme that they name: `expert_ids`: each row names 2 different experts; within the rows of one index of dp (aligned blocks of 3940 rows) no expert is named by more than 1232 rows, and in some such block one is named by exactly 1232.
All inputs are finite; a program needn't handle non-finite values.
Results may differ from a plain program's by a relative error of at most 0.015.
Values may be sent and summed in bfloat16 or wider, within the bound.
A program may use at most 192 MiB of HBM per device.

v0:
```python
import functools

import jax
import jax.numpy as jnp
from jax import lax
from jax.experimental import pallas as pl
from jax.experimental.pallas import tpu as pltpu
from jax.sharding import Mesh
from jax.sharding import PartitionSpec as P

HEAD_DIM = 64
SEQ = 197
EPSILON = 1e-06
ALIGN = 16
WIN = 224
CHUNK = 256
BLOCKS = 4
NEG = -1e30
F32 = jnp.float32
BF16 = jnp.bfloat16
INV_ROOT_TAU = 0.3989422804014327
ALL = ("chip", "core", "tensor")
DP = ("chip", "core")
RING = ("chip", "tensor")
SWAP = [(0, 1), (1, 0)]
VMEM_LIMIT = 60 * 1024 * 1024


def nn(a, b):
    return lax.dot_general(a, b, (((1,), (0,)), ((), ())), preferred_element_type=F32)


def nt(a, b):
    return lax.dot_general(a, b, (((1,), (1,)), ((), ())), preferred_element_type=F32)


def tn(a, b):
    return lax.dot_general(a, b, (((0,), (0,)), ((), ())), preferred_element_type=F32)


def standardize(matrix):
    centre = matrix - jnp.mean(matrix, -1, keepdims=True)
    variance = jnp.mean(centre * centre, -1, keepdims=True)
    inverse = lax.rsqrt(variance + EPSILON)
    return centre * inverse, inverse


def norm_back(weighted, scaled, inverse):
    return inverse * (
        weighted
        - jnp.mean(weighted, -1, keepdims=True)
        - scaled * jnp.mean(weighted * scaled, -1, keepdims=True)
    )


def window(i):
    first = i * SEQ
    start = pl.multiple_of((first // ALIGN) * ALIGN, ALIGN)
    return start, first - start


def put(ref, start, keep, value):
    head = pl.ds(start, ALIGN)
    ref[head, :] = jnp.where(keep, value[:ALIGN], ref[head, :])
    ref[pl.ds(start + ALIGN, WIN - ALIGN), :] = value[ALIGN:]


def fill(dst, src, rows):
    padded = dst.shape[0]
    dst[padded - ALIGN :, :] = jnp.zeros((ALIGN, dst.shape[1]), dst.dtype)
    dst[0:rows, :] = src[...]


def masks(offset):
    row = lax.broadcasted_iota(jnp.int32, (WIN, 1), 0)
    col = lax.broadcasted_iota(jnp.int32, (1, WIN), 1)
    valid = (row >= offset) & (row < offset + SEQ)
    bias = jnp.where((col >= offset) & (col < offset + SEQ), 0.0, NEG).astype(F32)
    keep = lax.broadcasted_iota(jnp.int32, (ALIGN, 1), 0) >= offset
    return valid, bias, keep


class Place:
    def __init__(self):
        self.chips, self.span = lax.axis_size("chip"), lax.axis_size("tensor")
        self.length = self.chips // 2
        chip = lax.axis_index("chip")
        self.z, self.x, self.y = chip // 2, chip % 2, lax.axis_index("tensor")
        self.sends = []

    def slot(self, z, x, y):
        return (z * 2 + x) * self.span + y

    def links(self):
        return (
            (self.z > 0, {"chip": (self.z - 1) * 2 + self.x}),
            (self.z < self.length - 1, {"chip": (self.z + 1) * 2 + self.x}),
            (None, {"chip": self.z * 2 + 1 - self.x}),
            (None, {"tensor": 1 - self.y}),
        )

    def greet(self, extra=()):
        barrier = pltpu.get_barrier_semaphore()
        for guard, device in self.links() + tuple(extra):
            run(guard, lambda device=device: pl.semaphore_signal(
                barrier, inc=1, device_id=device, device_id_type=pl.DeviceIdType.MESH))
        edge = jnp.where(self.z > 0, 1, 0) + jnp.where(self.z < self.length - 1, 1, 0)
        pl.semaphore_wait(barrier, 2 + len(extra) + edge)

    def post(self, guard, src, dst, recv_sem, link):
        index = len(self.sends)
        edge, device = self.links()[link]
        guard = both(guard, edge)

        def make():
            return remote(src, dst, self.send.at[index], recv_sem, device)

        self.sends.append((guard, make))
        run(guard, lambda: make().start())

    def receive(self, guard, dst, recv_sem):
        run(guard, lambda: remote(dst, dst, self.send.at[0], recv_sem, self.links()[2][1]).wait_recv())

    def drain(self):
        for guard, make in self.sends:
            run(guard, lambda make=make: make().wait_send())


def remote(src, dst, send_sem, recv_sem, device):
    return pltpu.make_async_remote_copy(
        src_ref=src, dst_ref=dst, send_sem=send_sem, recv_sem=recv_sem,
        device_id=device, device_id_type=pl.DeviceIdType.MESH,
    )


class Spread(Place):
    def __init__(self, src, dst, send, recv, own_sem):
        super().__init__()
        self.src, self.dst, self.send, self.recv, self.own_sem = src, dst, send, recv, own_sem

    def start(self, guard, half, place, link, own=False):
        to = self.dst.at[self.slot(*place), half]
        self.post(guard, self.src.at[half] if own else to, to, self.recv.at[self.slot(*place), half], link)

    def arrive(self, guard, half, place):
        self.receive(guard, self.dst.at[self.slot(*place), half], self.recv.at[self.slot(*place), half])

    def enter(self, guard, z, own=False):
        for half, link in ((0, 2), (1, 3), (0, 3), (1, 2)):
            self.start(guard, half, (z, self.x, self.y), link, own)

    def cross(self, guard, z):
        for half, place, link in (
            (0, (z, 1 - self.x, self.y), 3),
            (1, (z, self.x, 1 - self.y), 2),
        ):
            self.arrive(guard, half, place)
            self.start(guard, half, place, link)

    def keep(self):
        return pltpu.make_async_copy(self.src, self.dst.at[self.slot(self.z, self.x, self.y)], self.own_sem)

    def steps(self):
        def first():
            self.keep().start()
            for link in (0, 1):
                for half in range(2):
                    self.start(None, half, (self.z, self.x, self.y), link, True)
            self.enter(None, self.z, True)

        def hop(d):
            for side, onward in ((-1, 1), (1, 0)):
                z = self.z + side * d
                guard = z >= 0 if side < 0 else z < self.length
                for half in range(2):
                    self.arrive(guard, half, (z, self.x, self.y))
                    self.start(guard, half, (z, self.x, self.y), onward)
                self.enter(guard, z)
            self.crossing(d - 1)

        def last():
            self.crossing(self.length - 1)
            for z in range(self.length):
                for half, place in (
                    (0, (z, self.x, 1 - self.y)),
                    (0, (z, 1 - self.x, 1 - self.y)),
                    (1, (z, 1 - self.x, self.y)),
                    (1, (z, 1 - self.x, 1 - self.y)),
                ):
                    self.arrive(None, half, place)
            self.drain()
            self.keep().wait()

        return [first] + [functools.partial(hop, d) for d in range(1, self.length)] + [last]

    def crossing(self, d):
        if d == 0:
            self.cross(None, self.z)
        else:
            self.cross(self.z - d >= 0, self.z - d)
            self.cross(self.z + d < self.length, self.z + d)


def accumulate(dst, src):
    def add(d, s):
        d[...] = (d[...].astype(F32) + s[...].astype(F32)).astype(d.dtype)

    if len(dst.shape) == 2:
        add(dst, src)
        return

    def body(i, carry):
        add(dst.at[i], src.at[i])
        return carry

    lax.fori_loop(0, dst.shape[0], body, 0)


class Reduce(Place):
    def __init__(self, src, first, second, third, out, send, recv1, recv2, recv3, own=None, own_sem=None):
        super().__init__()
        self.src, self.first, self.second, self.third, self.out = src, first, second, third, out
        self.send, self.recv1, self.recv2, self.recv3 = send, recv1, recv2, recv3
        self.own, self.own_sem = own, own_sem

    def target(self, k):
        picked = 0
        for z in range(self.length):
            order = sorted(range(self.length), key=lambda to: (-abs(to - z), to))
            picked = picked + jnp.where(self.z == z, order[k], 0)
        return picked

    def sides(self):
        return ((0, 3, 2, 1 - self.x, self.x), (1, 2, 3, 1 - self.y, self.y))

    def kept(self, half, z, q):
        return self.slot(z, q, self.y) if half == 0 else self.slot(z, self.x, q)

    def sent(self, half, z, q):
        return self.slot(z, q, 1 - self.y) if half == 0 else self.slot(z, 1 - self.x, q)

    def load(self, half, z, q):
        at = 2 * z + q
        return pltpu.make_async_copy(
            self.src.at[self.kept(half, z, q), half], self.own.at[half, at], self.own_sem.at[half, at]
        )

    def stage(self, k):
        z = self.target(k)
        for half, _, _, far, near in self.sides():
            for q in (far, near):
                self.load(half, z, q).start()

    def one(self, k):
        z = self.target(k)
        for half, link, _, far, near in self.sides():
            for q in (far, near):
                self.post(
                    None, self.src.at[self.sent(half, z, q), half], self.first.at[half, 2 * z + q],
                    self.recv1.at[half, 2 * z + q], link,
                )

    def join(self, half, z, q):
        at = 2 * z + q
        self.receive(None, self.first.at[half, at], self.recv1.at[half, at])
        if self.own is None:
            mine = self.src.at[self.kept(half, z, q), half]
        else:
            self.load(half, z, q).wait()
            mine = self.own.at[half, at]
        accumulate(self.first.at[half, at], mine)

    def two(self, k):
        z = self.target(k)
        for half, _, link, far, near in self.sides():
            self.join(half, z, far)
            self.post(
                None, self.first.at[half, 2 * z + far], self.second.at[half, z], self.recv2.at[half, z], link
            )
        for half, _, link, far, near in self.sides():
            self.join(half, z, near)

    def three(self, k):
        z = self.target(k)
        left, right = self.z > 0, self.z < self.length - 1
        for half, _, _, _, near in self.sides():
            run_sum = self.second.at[half, z]
            self.receive(None, run_sum, self.recv2.at[half, z])
            accumulate(run_sum, self.first.at[half, 2 * z + near])
            for guard, more, link, at in (
                (z < self.z, right, 0, jnp.where(z == self.z - 1, self.length, z)),
                (z > self.z, left, 1, z),
            ):
                def take(half=half, run_sum=run_sum):
                    self.receive(None, self.third.at[half, z], self.recv3.at[half, z])
                    accumulate(run_sum, self.third.at[half, z])

                run(guard & more, take)
                self.post(guard, run_sum, self.third.at[half, at], self.recv3.at[half, at], link)

            def settle(half=half, run_sum=run_sum):
                out = self.out.at[half]
                out[...] = run_sum[...].astype(out.dtype)
                for guard, at in ((left, z), (right, self.length)):
                    def take(at=at):
                        self.receive(None, self.third.at[half, at], self.recv3.at[half, at])
                        accumulate(out, self.third.at[half, at])

                    run(guard, take)

            run(z == self.z, settle)


def reduce_sems(length):
    return [
        pltpu.SemaphoreType.DMA((10 * length,)),
        pltpu.SemaphoreType.DMA((2, 2 * length)),
        pltpu.SemaphoreType.DMA((2, length)),
        pltpu.SemaphoreType.DMA((2, length + 1)),
    ]


def reduce_room(length, block, dtype):
    return [pltpu.VMEM((2, n) + block, dtype) for n in (2 * length, length, length + 1)]


def both(a, b):
    if a is None or b is None:
        return b if a is None else a
    return a & b


def run(guard, body):
    if guard is None:
        body()
    else:
        pl.when(guard)(body)


def spread_sems(chips, span):
    length = chips // 2
    return [
        pltpu.SemaphoreType.DMA((8 + (2 * length - 2) * 6 + (2 * length - 1) * 2 + 8,)),
        pltpu.SemaphoreType.DMA((chips * span, 2)),
        pltpu.SemaphoreType.DMA,
    ]


def gather_small(src, wqkv_o, wout_o, par_o, dst, big, send, recv, own_sem, core_sem):
    core = lax.axis_index("core")
    sibling = {"core": 1 - core}
    spread = Spread(src, dst.at[core], send, recv, own_sem)
    spread.greet(((None, sibling),))
    for step in spread.steps():
        step()
    remote(dst.at[core], dst.at[core], core_sem.at[0], core_sem.at[1], sibling).start()
    remote(dst.at[core], dst.at[core], core_sem.at[0], core_sem.at[1], sibling).wait_send()
    remote(dst.at[1 - core], dst.at[1 - core], core_sem.at[0], core_sem.at[1], sibling).wait_recv()
    width, span = wqkv_o.shape[0], spread.span
    part, wide = width // (2 * spread.chips), width // span
    for group in range(2 * spread.chips):
        at = slice(part * group, part * (group + 1))
        for t in range(span):
            slot = (group // 2) * span + t
            piece = jnp.concatenate([dst[group % 2, slot, 0], dst[group % 2, slot, 1]], -1).astype(F32)[:part]
            for k in range(4):
                big[at, width * k + wide * t : width * k + wide * (t + 1)] = piece[:, wide * k : wide * (k + 1)]
            if t == 0:
                big[at, 4 * width : 4 * width + 128] = piece[:, 4 * wide : 4 * wide + 128]
    wqkv_o[...] = big[:, : 3 * width].astype(BF16)
    wout_o[...] = big[:, 3 * width : 4 * width].astype(BF16)
    par_o[...] = big[:, 4 * width : 4 * width + 128].T[0:8]


def attention_forward(
    tok, wqkv, wout, par, shard, normed_o, hidden_o, packed_o, mixed_o, lse_o, all_o, xs, send, recv, own_sem
):
    rows, width = tok.shape
    spread = Spread(shard, all_o, send, recv, own_sem)
    spread.greet()
    first, *rest = spread.steps()
    first()
    fill(xs, tok, rows)
    lane = lax.broadcasted_iota(jnp.int32, (1, 128), 1)
    low = lane < HEAD_DIM
    gain1, shift1, gain2, shift2 = (par[k : k + 1, :] for k in range(4))

    def image(i, carry):
        start, offset = window(i)
        valid, bias, keep = masks(offset)
        x = xs[pl.ds(start, WIN), :].astype(F32)
        scaled1, _ = standardize(x)
        normed1 = (scaled1 * gain1 + shift1).astype(BF16)
        packed = nn(normed1, wqkv[...]).astype(BF16)
        pieces = []
        lse = jnp.zeros((WIN, 128), F32)
        for pair in range(width // 128):
            at = 128 * pair
            q2 = packed[:, at : at + 128]
            k2 = packed[:, width + at : width + at + 128]
            v2 = packed[:, 2 * width + at : 2 * width + at + 128]
            halves = []
            for half in range(2):
                mine = low if half == 0 else ~low
                qm = jnp.where(mine, q2, jnp.zeros_like(q2)) * jnp.asarray(0.125, BF16)
                s = nt(qm, k2) + bias
                top = jnp.max(s, -1, keepdims=True)
                e = jnp.exp(s - top)
                total = jnp.sum(e, -1, keepdims=True)
                halves.append(nn(e.astype(BF16), v2) * (1.0 / total))
                lse = jnp.where(lane == 2 * pair + half, top + jnp.log(total), lse)
            pieces.append(jnp.where(low, halves[0], halves[1]).astype(BF16))
        mixed = jnp.concatenate(pieces, -1)
        hidden = x + nt(mixed, wout[...])
        scaled2, _ = standardize(hidden)
        put(normed_o, start, keep, (scaled2 * gain2 + shift2).astype(BF16))
        put(hidden_o, start, keep, hidden)
        put(packed_o, start, keep, packed)
        put(mixed_o, start, keep, mixed)
        put(lse_o, start, keep, lse)
        return carry

    images = rows // SEQ
    lax.fori_loop(0, images // 2, image, 0)
    rest[0]()
    lax.fori_loop(images // 2, images, image, 0)
    for step in rest[1:]:
        step()


def attention_backward(
    custom, tok, cot, hidden_r, packed_r, mixed_r, lse_r, own, other, wqkv, wout, par, grads,
    out_o, gtok_o, *refs,
):
    if custom:
        (
            gshard_o, small_o, xs, cs, outs, gtoks, gqkv_o, gout_o, gpar_o, pile, theirs,
            w_own, w1, w2, w3, s1, s2, s3, w_send, w_r1, w_r2, w_r3, w_own_sem,
            s_send, s_r1, s_r2, s_r3, core_sem,
        ) = refs
        core = lax.axis_index("core")
        sibling = {"core": 1 - core}
        big = Reduce(grads, w1, w2, w3, gshard_o, w_send, w_r1, w_r2, w_r3, w_own, w_own_sem)
        little = Reduce(pile.at[core], s1, s2, s3, small_o, s_send, s_r1, s_r2, s_r3)
        big.greet(((None, sibling),))
        ranks = range(big.length)
        big.one(0)
        big.one(1)
        for k in ranks:
            big.stage(k)
    else:
        gqkv_o, gout_o, gpar_o, xs, cs, outs, gtoks = refs
    rows, width = tok.shape
    fill(xs, tok, rows)
    fill(cs, cot, rows)
    gqkv_o[...] = jnp.zeros_like(gqkv_o)
    gout_o[...] = jnp.zeros_like(gout_o)
    gpar_o[...] = jnp.zeros_like(gpar_o)
    lane = lax.broadcasted_iota(jnp.int32, (1, 128), 1)
    low = lane < HEAD_DIM
    gain1, shift1, gain2 = (par[k : k + 1, :] for k in range(3))
    eighth = jnp.asarray(0.125, BF16)

    def image(i, carry):
        start, offset = window(i)
        valid, bias, keep = masks(offset)
        here = pl.ds(start, WIN)
        hidden = hidden_r[here, :]
        put(
            outs, start, keep,
            (hidden + own[here, 0:width].astype(F32) + other[here, 0:width].astype(F32)).astype(BF16),
        )
        scaled2, inverse2 = standardize(hidden)
        g2 = own[here, width:].astype(F32) + other[here, width:].astype(F32)
        g2 = jnp.where(valid, g2, 0.0)
        gpar_o[2:3, :] += jnp.sum(g2 * scaled2, 0, keepdims=True)
        gpar_o[3:4, :] += jnp.sum(g2, 0, keepdims=True)
        ghid = cs[here, :].astype(F32) + norm_back(g2 * gain2, scaled2, inverse2)
        branch = jnp.where(valid, ghid, 0.0).astype(BF16)
        gout_o[...] += tn(branch, mixed_r[here, :])
        gmix = nn(branch, wout[...]).astype(BF16)
        gq, gk, gv = [], [], []
        for pair in range(width // 128):
            at = 128 * pair
            q2 = packed_r[here, at : at + 128]
            k2 = packed_r[here, width + at : width + at + 128]
            v2 = packed_r[here, 2 * width + at : 2 * width + at + 128]
            gm2 = gmix[:, at : at + 128]
            sums = [0.0, 0.0, 0.0]
            for half in range(2):
                mine = low if half == 0 else ~low
                qm = jnp.where(mine, q2, jnp.zeros_like(q2)) * eighth
                km = jnp.where(mine, k2, jnp.zeros_like(k2)) * eighth
                gm = jnp.where(mine, gm2, jnp.zeros_like(gm2))
                head = 2 * pair + half
                lse = jnp.where(valid, lse_r[here, head : head + 1], -NEG)
                p = jnp.exp(nt(qm, k2) + bias - lse)
                gp = nt(gm, v2)
                inner = jnp.sum(gp * p, -1, keepdims=True)
                gs = (p * (gp - inner)).astype(BF16)
                sums[0] += nn(gs, km)
                sums[1] += tn(gs, qm)
                sums[2] += tn(p.astype(BF16), gm)
            for store, total in zip((gq, gk, gv), sums):
                store.append(total.astype(BF16))
        gpacked = jnp.concatenate(gq + gk + gv, -1)
        scaled1, inverse1 = standardize(xs[here, :].astype(F32))
        normed1 = (scaled1 * gain1 + shift1).astype(BF16)
        gqkv_o[...] += tn(normed1, gpacked)
        g1 = nt(gpacked, wqkv[...])
        gpar_o[0:1, :] += jnp.sum(g1 * scaled1, 0, keepdims=True)
        gpar_o[1:2, :] += jnp.sum(g1, 0, keepdims=True)
        put(gtoks, start, keep, ghid + norm_back(g1 * gain1, scaled1, inverse1))
        return carry

    images = rows // SEQ

    def finish():
        out_o[...] = outs[0:rows, :]
        gtok_o[...] = gtoks[0:rows, :]

    if not custom:
        lax.fori_loop(0, images, image, 0)
        finish()
        return

    lax.fori_loop(0, 3, image, 0)
    big.two(0)
    big.one(2)
    lax.fori_loop(3, 6, image, 0)
    big.two(1)
    big.one(3)
    lax.fori_loop(6, 8, image, 0)
    big.three(0)
    lax.fori_loop(8, images, image, 0)
    span = big.span
    part, wide = width // (2 * big.chips), width // span
    vectors = gpar_o[...].T
    for t in range(span):
        table = jnp.concatenate(
            [gqkv_o[:, width * k + wide * t : width * k + wide * (t + 1)] for k in range(3)]
            + [gout_o[:, wide * t : wide * (t + 1)], vectors, jnp.zeros_like(vectors)],
            -1,
        )
        for group in range(2 * big.chips):
            for half in range(2):
                pile[group % 2, (group // 2) * span + t, half] = table[
                    part * group : part * (group + 1), 512 * half : 512 * (half + 1)
                ]
    def across():
        return remote(pile.at[1 - core], theirs, core_sem.at[0], core_sem.at[1], sibling)

    across().start()
    big.two(2)
    big.three(1)
    finish()
    across().wait()

    def merge(i, carry):
        accumulate(pile.at[core, i, 0], theirs.at[i, 0])
        accumulate(pile.at[core, i, 1], theirs.at[i, 1])
        return carry

    lax.fori_loop(0, theirs.shape[0], merge, 0)
    for k in ranks:
        little.one(k)
    big.two(3)
    big.three(2)
    for k in ranks:
        little.two(k)
    big.three(3)
    for k in ranks:
        little.three(k)
    big.drain()
    little.drain()


def gelu_parts(v):
    e = jnp.exp(v * v * -0.5)
    t = 1.0 / (1.0 + jnp.abs(v) * (0.3275911 * 0.7071067811865476))
    q = 0.5 * 1.061405429
    for c in (-1.453152027, 1.421413741, -0.284496736, 0.254829592):
        q = q * t + 0.5 * c
    q = q * t * e
    return jnp.where(v < 0, q, 1.0 - q), e * INV_ROOT_TAU


def experts(
    cnt, rown, rsib, cown, csib, town, tsib, w_ref,
    pown, psib, g_ref, xb, gb, tmpx, tmpg, acc1, acc2, off, dst, base, tot,
):
    number = pl.num_programs(0)
    e_now = pl.program_id(0)
    depth = town.shape[2]
    width = rown.shape[1]
    slots = tmpx.shape[0]
    step = slots // 3

    def blocks(fn):
        for side, (table, r, c, out) in enumerate(((town, rown, cown, pown), (tsib, rsib, csib, psib))):
            def body(j, carry, side=side, table=table, r=r, c=c, out=out):
                fn(side * BLOCKS + j, table[j], r, c, out, pl.ds(pl.multiple_of(j * depth, ALIGN), depth))
                return carry

            lax.fori_loop(0, BLOCKS, body, 0)

    def onehot(table, at):
        slot = (lax.broadcasted_iota(jnp.int32, (step, 1), 0) + at).astype(F32)
        first = table[0:1, :] == slot
        second = table[1:2, :] == slot
        gate = jnp.where(first, table[2:3, :], jnp.where(second, table[3:4, :], 0.0))
        pick = jnp.where(first | second, 1.0, 0.0).astype(BF16)
        return pick, jnp.sum(gate, -1, keepdims=True)

    def segments(b, move):
        def per(e, carry):
            k = b * number + e
            o, d = off[k], dst[k]

            def tile(t, carry):
                move(
                    pl.ds(pl.multiple_of(o + t * ALIGN, ALIGN), ALIGN),
                    pl.ds(pl.multiple_of(d + t * ALIGN, ALIGN), ALIGN),
                )
                return carry

            return lax.fori_loop(0, (cnt[k] + (ALIGN - 1)) // ALIGN, tile, carry)

        lax.fori_loop(0, number, per, 0)

    @pl.when(e_now == 0)
    def _():
        def plan_expert(e, at):
            base[e] = at

            def plan_block(b, run):
                dst[b * number + e] = at + run
                return run + (cnt[b * number + e] + (ALIGN - 1)) // ALIGN * ALIGN

            total = lax.fori_loop(0, 2 * BLOCKS, plan_block, 0)
            tot[e] = total
            return at + (total + (CHUNK - 1)) // CHUNK * CHUNK

        lax.fori_loop(0, number, plan_expert, 0)

        def plan_off(b, carry):
            def one(e, run):
                off[b * number + e] = run
                return run + (cnt[b * number + e] + (ALIGN - 1)) // ALIGN * ALIGN

            lax.fori_loop(0, number, one, 0)
            return carry

        lax.fori_loop(0, 2 * BLOCKS, plan_off, 0)

        def dispatch(b, table, r, c, out, here):
            rows, cots = r[here, :], c[here, :]
            for k in range(3):
                pick, gate = onehot(table, k * step)
                tmpx[k * step : (k + 1) * step, :] = nn(pick, rows).astype(BF16)
                tmpg[k * step : (k + 1) * step, :] = (nn(pick, cots) * gate).astype(BF16)

            def move(local, far):
                xb[far, :] = tmpx[local, :]
                gb[far, :] = tmpg[local, :]

            segments(b, move)

        blocks(dispatch)

        def clear(e, carry):
            total = tot[e]
            end = base[e] + total

            def tile(t, carry):
                far = pl.ds(pl.multiple_of(end + t * ALIGN, ALIGN), ALIGN)
                xb[far, :] = jnp.zeros((ALIGN, width), BF16)
                gb[far, :] = jnp.zeros((ALIGN, width), BF16)
                return carry

            rest = (total + (CHUNK - 1)) // CHUNK * CHUNK - total
            return lax.fori_loop(0, rest // ALIGN, tile, carry)

        lax.fori_loop(0, number, clear, 0)

    shards, units = w_ref.shape[0], w_ref.shape[2] // 2
    hidden = shards * units
    acc1[...] = jnp.zeros_like(acc1)
    acc2[...] = jnp.zeros_like(acc2)

    def chunk(t, carry):
        here = pl.ds(pl.multiple_of(base[e_now] + t * CHUNK, ALIGN), CHUNK)
        first = w_ref[:, 0, 0:units].reshape(hidden, width)
        second = w_ref[:, 0, units:].reshape(hidden, width)
        x, g = xb[here, :], gb[here, :]
        v = nt(x, first)
        big, small = gelu_parts(v)
        act = (v * big).astype(BF16)
        gpre = (nt(g, second) * (big + v * small)).astype(BF16)
        acc1[...] += tn(gpre, x)
        acc2[...] += tn(act, g)
        xb[here, :] = nn(act, second).astype(BF16)
        gb[here, :] = nn(gpre, first).astype(BF16)
        return carry

    lax.fori_loop(0, (tot[e_now] + (CHUNK - 1)) // CHUNK, chunk, 0)
    g_ref[:, 0, 0:units] = acc1[...].reshape(shards, units, width).astype(BF16)
    g_ref[:, 0, units:] = acc2[...].reshape(shards, units, width).astype(BF16)

    @pl.when(e_now == number - 1)
    def _():
        def combine(b, table, r, c, out, here):
            def move(local, far):
                tmpx[local, :] = xb[far, :]
                tmpg[local, :] = gb[far, :]

            segments(b, move)
            forward, back = 0.0, 0.0
            for k in range(3):
                pick, gate = onehot(table, k * step)
                part = slice(k * step, (k + 1) * step)
                forward += tn(pick, (tmpx[part, :].astype(F32) * gate).astype(BF16))
                back += tn(pick, tmpg[part, :])
            out[here, 0:width] = forward.astype(BF16)
            out[here, width:] = back.astype(BF16)

        blocks(combine)


def route(ids, gates, number, padded):
    rows = ids.shape[1]
    depth = padded // BLOCKS
    ids = jnp.pad(ids, ((0, 0), (0, padded - rows)), constant_values=-1)
    gates = jnp.pad(gates, ((0, 0), (0, padded - rows)))
    ids = ids.reshape(2, BLOCKS, 1, depth)
    gates = gates.reshape(2, BLOCKS, 1, depth)
    match = ids == jnp.arange(number, dtype=jnp.int32)[None, None, :, None]
    named = (match[0] | match[1]).astype(BF16)
    order = jnp.arange(depth)
    earlier = (order[:, None] < order[None, :]).astype(BF16)
    rank = jnp.einsum("ber,rs->bes", named, earlier, preferred_element_type=F32)
    count = jnp.sum(named.astype(F32), -1)
    room = jnp.ceil(count * (1.0 / ALIGN)) * ALIGN
    before = jnp.arange(number)
    off = jnp.sum(jnp.where(before[None, :, None] < before[None, None, :], room[:, :, None], 0.0), 1)
    place = off[:, :, None] + rank
    slot = jnp.sum(jnp.where(match, place[None], 0.0), 2)
    slot = jnp.where(ids[:, :, 0] >= 0, slot, -1.0)
    table = jnp.stack([slot[0], slot[1], gates[0, :, 0], gates[1, :, 0]], 1)
    lanes = jnp.pad(count, ((0, 0), (0, depth - number)))
    return jnp.concatenate([table, lanes[:, None, :], jnp.zeros((BLOCKS, 3, depth), F32)], 1)


def whole(shape, dtype):
    return jax.ShapeDtypeStruct(shape, dtype)


IN_VMEM = pl.BlockSpec(memory_space=pltpu.VMEM)


def on_device(
    tokens, query_key_value, attention_out, first_gain, first_shift, second_gain, second_shift,
    expert_in, expert_out, expert_ids, gate_weights, cotangent,
):
    rows, width = tokens.shape
    padded = -(-rows // (ALIGN * BLOCKS)) * (ALIGN * BLOCKS)
    number = expert_in.shape[0]
    groups, span = lax.axis_size(DP), lax.axis_size("tensor")
    part = width // groups
    wide = width // span
    half = lax.axis_index("tensor")

    chips = groups // 2
    slots_all = chips * span
    custom = chips == 8 and span == 2 and part % 8 == 0
    vectors = jnp.stack([first_gain, first_shift, second_gain, second_shift], 1)
    small = jnp.concatenate(
        [
            query_key_value.reshape(part, 3 * wide),
            attention_out.T,
            jnp.pad(vectors, ((0, 0), (0, 1024 - 4 * wide - 4))),
        ],
        1,
    )
    shard = jnp.concatenate([expert_in.transpose(0, 2, 1), expert_out], 1)
    shards, units = slots_all, shard.shape[1] // 2
    if custom:
        lines = -(-part // ALIGN) * ALIGN
        wqkv, wout, par = pl.pallas_call(
            gather_small,
            out_shape=(
                whole((width, 3 * width), BF16),
                whole((width, width), BF16),
                whole((8, width), F32),
            ),
            in_specs=[IN_VMEM],
            out_specs=(IN_VMEM,) * 3,
            scratch_shapes=[
                pltpu.VMEM((2, slots_all, 2, lines, 512), BF16),
                pltpu.VMEM((width, 4 * width + 128), F32),
            ]
            + spread_sems(chips, span)
            + [pltpu.SemaphoreType.DMA((2,))],
            compiler_params=pltpu.CompilerParams(collective_id=0, has_side_effects=True, vmem_limit_bytes=VMEM_LIMIT),
            name="gather_small",
        )(jnp.pad(small, ((0, lines - part), (0, 0))).reshape(lines, 2, 512).transpose(1, 0, 2))
    else:
        gathered = lax.all_gather(small, ALL, axis=0, tiled=False).reshape(groups, span, part, 1024)
        taken = gathered[..., : 4 * wide].reshape(groups, span, part, 4, wide)
        taken = taken.transpose(0, 2, 3, 1, 4).reshape(width, 4, width)
        wqkv, wout = taken[:, :3].reshape(width, 3 * width), taken[:, 3]
        par = gathered[:, 0, :, 4 * wide : 4 * wide + 8].reshape(width, 8).T.astype(F32)

    ids = lax.dynamic_slice_in_dim(expert_ids.T, half * rows, rows, 1)
    gates = lax.dynamic_slice_in_dim(gate_weights.T, half * rows, rows, 1)
    table = route(ids, gates, number, padded)
    table_sib = lax.ppermute(table, "core", SWAP)
    cot_own = jnp.pad(cotangent, ((0, padded - rows), (0, 0)))
    cot_sib = lax.ppermute(cot_own, "core", SWAP)

    normed, hidden, packed, mixed, lse, weights = pl.pallas_call(
        attention_forward,
        out_shape=(
            whole((padded, width), BF16),
            whole((padded, width), F32),
            whole((padded, 3 * width), BF16),
            whole((padded, width), BF16),
            whole((padded, 128), F32),
            whole((shards, 2, number // 2, 2 * units, width), BF16),
        ),
        in_specs=[IN_VMEM] * 5,
        out_specs=(IN_VMEM,) * 5 + (pl.BlockSpec(memory_space=pl.ANY),),
        scratch_shapes=[pltpu.VMEM((padded, width), BF16)] + spread_sems(chips, span),
        compiler_params=pltpu.CompilerParams(vmem_limit_bytes=VMEM_LIMIT, collective_id=1, has_side_effects=True),
        cost_estimate=pl.CostEstimate(flops=6 * 10**9, bytes_accessed=14 * 10**6, transcendentals=3 * 10**6),
        name="attention_forward",
    )(tokens, wqkv, wout, par, shard.reshape(2, number // 2, 2 * units, width))
    weights = weights.reshape(shards, number, 2 * units, width)
    regroup = units % ALIGN != 0
    if regroup:
        weights = weights.reshape(shards, number, 2, units, width)
        weights = weights.transpose(1, 2, 0, 3, 4).reshape(1, number, 2 * shards * units, width)
    normed_sib = lax.ppermute(normed, "core", SWAP)

    counts = jnp.concatenate([table[:, 4, :number], table_sib[:, 4, :number]], 0).astype(jnp.int32).reshape(-1)
    n_blocks = 2 * BLOCKS
    room = -(-(4 * rows + n_blocks * number * (ALIGN - 1) + number * (CHUNK - ALIGN)) // CHUNK) * CHUNK
    depth = padded // BLOCKS
    slots = -(-(2 * depth + number * (ALIGN - 1)) // (3 * ALIGN)) * (3 * ALIGN)
    held = weights.shape[0] * weights.shape[2] // 2

    def full(*shape):
        return pl.BlockSpec(shape, lambda e, *_: (0,) * len(shape), pipeline_mode=pl.Buffered(1))

    by_expert = pl.BlockSpec(
        (weights.shape[0], 1, weights.shape[2], width), lambda e, *_: (0, e, 0, 0)
    )
    part_own, part_sib, grads = pl.pallas_call(
        experts,
        out_shape=(
            whole((padded, 2 * width), BF16),
            whole((padded, 2 * width), BF16),
            whole(weights.shape, BF16),
        ),
        grid_spec=pltpu.PrefetchScalarGridSpec(
            num_scalar_prefetch=1,
            grid=(number,),
            in_specs=[full(padded, width)] * 4 + [full(*table.shape)] * 2 + [by_expert],
            out_specs=(full(padded, 2 * width), full(padded, 2 * width), by_expert),
            scratch_shapes=[
                pltpu.VMEM((room, width), BF16),
                pltpu.VMEM((room, width), BF16),
                pltpu.VMEM((slots, width), BF16),
                pltpu.VMEM((slots, width), BF16),
                pltpu.VMEM((held, width), F32),
                pltpu.VMEM((held, width), F32),
                pltpu.SMEM((n_blocks * number,), jnp.int32),
                pltpu.SMEM((n_blocks * number,), jnp.int32),
                pltpu.SMEM((number,), jnp.int32),
                pltpu.SMEM((number,), jnp.int32),
            ],
        ),
        compiler_params=pltpu.CompilerParams(
            vmem_limit_bytes=VMEM_LIMIT, dimension_semantics=("arbitrary",)
        ),
        cost_estimate=pl.CostEstimate(flops=50 * 10**9, bytes_accessed=40 * 10**6, transcendentals=12 * 10**6),
        name="experts",
    )(counts, normed, normed_sib, cot_own, cot_sib, table, table_sib, weights)
    part_other = lax.ppermute(part_sib, "core", SWAP)
    if regroup:
        grads = grads.reshape(number, 2, shards, units, width).transpose(2, 0, 1, 3, 4)
        grads = grads.reshape(shards, number, 2 * units, width)

    sums = [
        pltpu.VMEM((width, 3 * width), F32),
        pltpu.VMEM((width, width), F32),
        pltpu.VMEM((128, width), F32),
    ]
    rows_scratch = [
        pltpu.VMEM((padded, width), BF16),
        pltpu.VMEM((padded, width), BF16),
        pltpu.VMEM((padded, width), BF16),
        pltpu.VMEM((padded, width), F32),
    ]
    operands = (tokens, cotangent, hidden, packed, mixed, lse, part_own, part_other, wqkv, wout, par)
    shapes = (whole((rows, width), BF16), whole((rows, width), F32))
    estimate = pl.CostEstimate(flops=15 * 10**9, bytes_accessed=25 * 10**6, transcendentals=3 * 10**6)
    if custom:
        length = chips // 2
        block, tile = (number // 2, 2 * units, width), (part, 512)
        output, grad_tokens, grad_shard, mine = pl.pallas_call(
            functools.partial(attention_backward, True),
            out_shape=shapes + (whole((2,) + block, F32), whole((2,) + tile, F32)),
            in_specs=[IN_VMEM] * 11 + [pl.BlockSpec(memory_space=pl.ANY)],
            out_specs=(IN_VMEM,) * 4,
            scratch_shapes=rows_scratch
            + sums
            + [pltpu.VMEM((2, shards, 2) + tile, F32), pltpu.VMEM((shards, 2) + tile, F32)]
            + [pltpu.VMEM((2, 2 * length) + block, BF16)]
            + reduce_room(length, block, BF16)
            + reduce_room(length, tile, F32)
            + reduce_sems(length)
            + [pltpu.SemaphoreType.DMA((2, 2 * length))]
            + reduce_sems(length)
            + [pltpu.SemaphoreType.DMA((2,))],
            compiler_params=pltpu.CompilerParams(
                vmem_limit_bytes=VMEM_LIMIT, collective_id=2, has_side_effects=True
            ),
            cost_estimate=estimate,
            name="attention_backward",
        )(*operands, grads.reshape((shards, 2) + block))
        mine = mine.transpose(1, 0, 2).reshape(part, 1024)
        grad_shard = grad_shard.reshape(number, 2 * units, width)
    else:
        output, grad_tokens, gqkv, gout, gpar = pl.pallas_call(
            functools.partial(attention_backward, False),
            out_shape=shapes + tuple(whole(ref.shape, F32) for ref in sums),
            in_specs=[IN_VMEM] * 11 + [pl.BlockSpec(memory_space=pl.ANY)],
            out_specs=(IN_VMEM,) * 5,
            scratch_shapes=rows_scratch,
            compiler_params=pltpu.CompilerParams(vmem_limit_bytes=VMEM_LIMIT),
            cost_estimate=estimate,
            name="attention_backward",
        )(*operands, grads)
        grad_shard = lax.psum_scatter(grads, RING, scatter_dimension=0, tiled=False).astype(F32)
        owed = jnp.concatenate([gqkv.reshape(width, 3, width), gout[:, None]], 1)
        owed = owed.reshape(groups, part, 4, span, wide).transpose(0, 3, 1, 2, 4)
        owed = owed.reshape(groups, span, part, 4 * wide)
        own_vectors = jnp.broadcast_to(gpar[:8].T.reshape(groups, 1, part, 8), (groups, span, part, 8))
        owed = jnp.concatenate([owed, own_vectors], -1).reshape(groups * span, part, 4 * wide + 8)
        mine = lax.psum_scatter(owed, ALL, scatter_dimension=0, tiled=False)
    vectors = mine[:, 4 * wide : 4 * wide + 4]
    return (
        output,
        grad_tokens,
        mine[:, : 3 * wide].reshape(part, 3, wide),
        mine[:, 3 * wide : 4 * wide].T,
        vectors[:, 0],
        vectors[:, 1],
        vectors[:, 2],
        vectors[:, 3],
        grad_shard[:, :units].transpose(0, 2, 1),
        grad_shard[:, units:],
    )


def solution(mesh):
    groups, span = mesh.devices.shape
    split = Mesh(mesh.devices.reshape(groups // 2, 2, span), ALL)
    return jax.shard_map(
        on_device,
        mesh=split,
        in_specs=(
            P(ALL, None),
            P(DP, None, "tensor"),
            P("tensor", DP),
            P(DP),
            P(DP),
            P(DP),
            P(DP),
            P(None, None, ALL),
            P(None, ALL, None),
            P(DP, None),
            P(DP, None),
            P(ALL, None),
        ),
        out_specs=(
            P(ALL, None),
            P(ALL, None),
            P(DP, None, "tensor"),
            P("tensor", DP),
            P(DP),
            P(DP),
            P(DP),
            P(DP),
            P(None, None, ALL),
            P(None, ALL, None),
        ),
        check_vma=False,
    )
```

profile of v0, /device:TPU:0, one launch (start us, length us, event | category | flops | bytes accessed | tf_op | source)
XLA Modules:
  0.0 373.1 jit_solution(13542590232142412821)
XLA Ops:
  0.6 0.0 copy-start
  0.7 0.0 copy-start.10
  0.7 0.0 copy-start.11
  0.7 1.6 pad.29.cown
  2.4 0.6 collective-permute-start.2
  2.9 0.0 copy-done.13
  3.0 0.1 copy.41
  3.1 0.0 copy-done.7
  3.1 0.1 reshape.77
  3.2 0.1 fusion.4
  3.3 0.6 copy.52
  3.9 25.5 %gather_small.1 = (bf16[384,1152]{1,0:T(8,128)(2,1)}, bf16[384,384]{1,0:T(8,128)(2,1)}, f32[8,384]{1,0:T(8,128)}) custom-call(bf16[2,32,512]{2,1,0:T(8,128)(2,1)} %bitcast.49), custom_call_target="tpu_custom_call" | custom-call | tf_op jit(solution)/shard_map/gather_small/pallas_call | solution.py:789
  29.4 0.9 pad_maximum_fusion
  30.3 88.1 %attention_forward.1 = (bf16[1984,384]{1,0:T(8,128)(2,1)}, f32[1984,384]{1,0:T(8,128)}, bf16[1984,1152]{1,0:T(8,128)(2,1)}, bf16[1984,384]{1,0:T(8,128)(2,1)}, f...) custom-call(bf16[1970,384]{1,0:T(8,128)(2,1)} %tok.3, bf16[384,1152]{1,0:T(8,128)(2,1)} %get-tuple-element.26.wqkv, ...), custom_call_target="tpu_custom_call" | custom-call | flops 6000000000 | bytes 14000000 | tf_op jit(solution)/shard_map/attention_forward/pallas_call | solution.py:821
  118.4 0.1 collective-permute-start.1
  118.5 0.1 dynamic-slice_bitcast_fusion.1
  118.6 0.1 eq.15
  118.7 0.0 copy-done.9
  118.7 0.1 dynamic-slice_bitcast_fusion
  118.8 0.1 stack_squeeze.15
  118.9 0.1 stack_squeeze.14
  119.0 0.1 convert_reduce_fusion
  119.2 0.1 select_reduce_fusion.1
  119.3 0.2 convolution_add_fusion
  119.5 0.1 select_reduce_fusion
  119.6 0.1 concatenate.14.town
  119.7 0.0 copy-start.6
  119.7 0.5 collective-permute-start
  120.2 1.9 collective-permute-done.tsib
  122.1 0.6 convert_element_type.27.cnt
  122.7 0.0 collective-permute-done.2.csib
  122.7 0.0 collective-permute-done.1.rsib
  122.7 1.1 copy-done.16
  123.8 119.0 %experts.1 = (bf16[1984,768]{1,0:T(8,128)(2,1)}, bf16[1984,768]{1,0:T(8,128)(2,1)}, bf16[16,8,96,384]{3,2,1,0:T(8,128)(2,1)}) custom-call(s32[64]{0:T(128)} %convert_element_type.27.cnt, bf16[1984,384]{1,0:T(8,128)(2,1)} %get-tuple-element.33.rown, bf16[1984,384]{1,0:T(8,128)(2,1)} %copy-done.16, bf16[1984,384]{1,0:T(8,128)(2,1)} %copy-done.2, ...), custom_call_target="tpu_custom_call" | custom-call | flops 49999998976 | bytes 40000000 | tf_op jit(solution)/shard_map/experts/pallas_call | solution.py:858
  242.9 0.1 collective-permute-start.3
  243.0 5.6 %collective-permute-done.3.other = bf16[1984,768]{1,0:T(8,128)(2,1)S(1)} collective-permute-done((bf16[1984,768]{1,0:T(8,128)(2,1)}, bf16[1984,768]{1,0:T(8,128)(2,1)S(1)}, u32[]{:S(2)}, u32[]{:S(2)}) %collective-permute-start.3) | collective-permute-done | bytes 3047456 | tf_op jit(solution)/shard_map/ppermute | solution.py:889
  248.6 1.6 copy-done.15
  250.2 113.3 %attention_backward.1 = (bf16[1970,384]{1,0:T(8,128)(2,1)}, f32[1970,384]{1,0:T(8,128)}, f32[2,4,96,384]{3,2,1,0:T(8,128)}, f32[2,24,512]{2,1,0:T(8,128)}) custom-call(bf16[1970,384]{1,0:T(8,128)(2,1)} %tok.3, bf16[1970,384]{1,0:T(8,128)(2,1)} %cot.1, f32[1984,384]{1,0:T(8,128)} %get-tuple-element.29.hidden_r, ...), custom_call_target="tpu_custom_call" | custom-call | flops 15000000512 | bytes 25000000 | tf_op jit(solution)/shard_map/attention_backward/pallas_call | solution.py:911
  363.5 1.0 copy.48
  364.5 0.7 slice_reduce_fusion
  365.3 0.7 slice_bitcast_fusion.1
  365.9 0.1 reshape.83
  366.0 0.6 copy.46
  366.7 2.3 fusion.8
  369.0 0.0 copy-done.3
  369.0 1.1 copy.55
  370.2 1.3 copy-done.1
  371.4 1.6 copy.56
  (40 shorter events, 0.3 us)
Async XLA Ops:
  0.6 117.8 %copy-start = (s32[3940,2]{0,1:T(2,128)S(1)}, s32[3940,2]{0,1:T(2,128)}, u32[]{:S(2)}) copy-start(s32[3940,2]{0,1:T(2,128)} %param.21) | copy-start | bytes 94564
  0.7 2.3 copy-start.10
  0.7 2.3 copy-start.11
  0.7 2.2 copy-start.12
  0.7 2.2 copy-start.13
  0.7 2.4 copy-start.7
  0.7 2.5 copy-start.8
  0.7 28.7 %copy-start.4 = (bf16[8,48,384]{2,1,0:T(8,128)(2,1)S(1)}, bf16[8,48,384]{2,1,0:T(8,128)(2,1)}, u32[]{:S(2)}) copy-start(bf16[8,48,384]{2,1,0:T(8,128)(2,1)} %param.20) | copy-start | bytes 884740
  0.7 28.7 %copy-start.5 = (bf16[8,384,48]{1,2,0:T(8,128)(2,1)S(1)}, bf16[8,384,48]{1,2,0:T(8,128)(2,1)}, u32[]{:S(2)}) copy-start(bf16[8,384,48]{1,2,0:T(8,128)(2,1)} %param.19) | copy-start | bytes 884740
  2.4 116.0 %copy-start.2 = (bf16[1984,384]{1,0:T(8,128)(2,1)}, bf16[1984,384]{1,0:T(8,128)(2,1)S(1)}, u32[]{:S(2)}) copy-start(bf16[1984,384]{1,0:T(8,128)(2,1)S(1)} %pad.29.cown) | copy-start | bytes 4571140
  2.4 120.4 %collective-permute-start.2 = (bf16[1984,384]{1,0:T(8,128)(2,1)S(1)}, bf16[1984,384]{1,0:T(8,128)(2,1)}, u32[]{:S(2)}, u32[]{:S(2)}) collective-permute-start(bf16[1984,384]{1,0:T(8,128)(2,1)S(1)} %pad.29.cown), channel_id=1, source_target_pairs={{0,2},{2,0},{1,3},{3,1},{4,6},{6,4},{5,7},{7,5},{8,10},{10,8},{9,1... | collective-permute-start | bytes 4571144 | tf_op jit(solution)/shard_map/ppermute | solution.py:819
  30.3 88.4 %copy-start.9 = (f32[3940,2]{0,1:T(2,128)S(1)}, f32[3940,2]{0,1:T(2,128)}, u32[]{:S(2)}) copy-start(f32[3940,2]{0,1:T(2,128)} %param.22) | copy-start | bytes 94564
  118.4 4.3 %collective-permute-start.1 = (bf16[1984,384]{1,0:T(8,128)(2,1)}, bf16[1984,384]{1,0:T(8,128)(2,1)S(1)}, u32[]{:S(2)}, u32[]{:S(2)}) collective-permute-start(bf16[1984,384]{1,0:T(8,128)(2,1)} %get-tuple-element.33.rown), channel_id=1, source_target_pairs={{0,2},{2,0},{1,3},{3,1},{4,6},{6,4},{5,7},{7,5},{8,10},{10,8},{9,1... | collective-permute-start | bytes 4571144 | tf_op jit(solution)/shard_map/ppermute | solution.py:843
  119.7 3.1 copy-start.6
  119.7 2.4 collective-permute-start
  122.1 0.6 copy-start.14
  122.7 1.1 copy-start.16
  242.9 5.7 %collective-permute-start.3 = (bf16[1984,768]{1,0:T(8,128)(2,1)}, bf16[1984,768]{1,0:T(8,128)(2,1)S(1)}, u32[]{:S(2)}, u32[]{:S(2)}) collective-permute-start(bf16[1984,768]{1,0:T(8,128)(2,1)} %get-tuple-element.36), channel_id=1, source_target_pairs={{0,2},{2,0},{1,3},{3,1},{4,6},{6,4},{5,7},{7,5},{8,10},{10,8},{9,1... | collective-permute-start | bytes 9142280 | tf_op jit(solution)/shard_map/ppermute | solution.py:889
  248.6 1.6 copy-start.15
  363.5 5.5 %copy-start.3 = (bf16[1970,384]{1,0:T(8,128)(2,1)S(1)}, bf16[1970,384]{1,0:T(8,128)(2,1)}, u32[]{:S(2)}) copy-start(bf16[1970,384]{1,0:T(8,128)(2,1)} %get-tuple-element.92) | copy-start | bytes 4538884
  369.0 2.4 copy-start.1
where the time goes:
time: 372 us; the launch traced here: 373 us
  Pallas kernels  346 us (93%)
  local copies, waits for them, and re-layouts  16 us (4%)
  waiting for transfers between devices  7.46 us (2%)
    pallas_call x1, Pallas kernels, on_device(): pl.pallas_call(experts, out_shape=(whole((padded, 2 * width), BF16), whol...  119 us
    pallas_call x1, Pallas kernels, on_device(): pl.pallas_call(functools.partial(attention_backward, True), out_shape=sha...  113 us
    pallas_call x1, Pallas kernels, on_device(): pl.pallas_call(attention_forward, out_shape=(whole((padded, width), BF16)...  88.1 us
    pallas_call x1, Pallas kernels, on_device(): pl.pallas_call(gather_small, out_shape=(whole((width, 3 * width), BF16),...  25.5 us
    unnamed x38, local copies, waits for them, and re-layouts  7.46 us
  transfers between devices with their start and end apart: 4, of which 2 were waited for; matrix products, arithmetic and copies ran while one was open for 1% of the time, Pallas kernels for 30%

commit v1 on v0

--- a/solution.py
+++ b/solution.py
@@ -15,6 +15,7 @@
 WIN = 224
 CHUNK = 256
 BLOCKS = 4
+STEP = 192
 NEG = -1e30
 F32 = jnp.float32
 BF16 = jnp.bfloat16
@@ -134,64 +135,67 @@
 
 
 class Spread(Place):
-    def __init__(self, src, dst, send, recv, own_sem):
+    def __init__(self, src, own, other, send, recv, keep_sem):
         super().__init__()
-        self.src, self.dst, self.send, self.recv, self.own_sem = src, dst, send, recv, own_sem
-
-    def start(self, guard, half, place, link, own=False):
-        to = self.dst.at[self.slot(*place), half]
-        self.post(guard, self.src.at[half] if own else to, to, self.recv.at[self.slot(*place), half], link)
-
-    def arrive(self, guard, half, place):
-        self.receive(guard, self.dst.at[self.slot(*place), half], self.recv.at[self.slot(*place), half])
-
-    def enter(self, guard, z, own=False):
-        for half, link in ((0, 2), (1, 3), (0, 3), (1, 2)):
-            self.start(guard, half, (z, self.x, self.y), link, own)
+        self.src, self.own, self.other = src, own, other
+        self.send, self.recv, self.keep_sem = send, recv, keep_sem
+
+    def sides(self):
+        return ((0, 2, 3, self.x), (1, 3, 2, self.y))
+
+    def start(self, guard, half, at, rel, link, fresh=False):
+        src = self.src[half] if fresh else self.own[half].at[at]
+        dst = (self.own, self.other)[rel][half].at[at]
+        self.post(guard, src, dst, self.recv.at[half, rel, at], link)
+
+    def arrive(self, guard, half, at, rel):
+        self.receive(guard, (self.own, self.other)[rel][half].at[at], self.recv.at[half, rel, at])
+
+    def enter(self, guard, z, fresh=False):
+        for half, near_link, far_link, near in self.sides():
+            self.start(guard, half, 2 * z + near, 0, near_link, fresh)
+        if self.other is not None:
+            for half, near_link, far_link, near in self.sides():
+                self.start(guard, half, 2 * z + near, 1, far_link, fresh)
 
     def cross(self, guard, z):
-        for half, place, link in (
-            (0, (z, 1 - self.x, self.y), 3),
-            (1, (z, self.x, 1 - self.y), 2),
-        ):
-            self.arrive(guard, half, place)
-            self.start(guard, half, place, link)
-
-    def keep(self):
-        return pltpu.make_async_copy(self.src, self.dst.at[self.slot(self.z, self.x, self.y)], self.own_sem)
-
-    def steps(self):
-        def first():
-            self.keep().start()
-            for link in (0, 1):
-                for half in range(2):
-                    self.start(None, half, (self.z, self.x, self.y), link, True)
-            self.enter(None, self.z, True)
-
-        def hop(d):
-            for side, onward in ((-1, 1), (1, 0)):
-                z = self.z + side * d
-                guard = z >= 0 if side < 0 else z < self.length
-                for half in range(2):
-                    self.arrive(guard, half, (z, self.x, self.y))
-                    self.start(guard, half, (z, self.x, self.y), onward)
-                self.enter(guard, z)
-            self.crossing(d - 1)
-
-        def last():
-            self.crossing(self.length - 1)
-            for z in range(self.length):
-                for half, place in (
-                    (0, (z, self.x, 1 - self.y)),
-                    (0, (z, 1 - self.x, 1 - self.y)),
-                    (1, (z, 1 - self.x, self.y)),
-                    (1, (z, 1 - self.x, 1 - self.y)),
-                ):
-                    self.arrive(None, half, place)
-            self.drain()
-            self.keep().wait()
-
-        return [first] + [functools.partial(hop, d) for d in range(1, self.length)] + [last]
+        for half, near_link, far_link, near in self.sides():
+            at = 2 * z + 1 - near
+            self.arrive(guard, half, at, 0)
+            if self.other is not None:
+                self.start(guard, half, at, 1, far_link)
+
+    def keep(self, half):
+        near = self.sides()[half][3]
+        return pltpu.make_async_copy(self.src[half], self.own[half].at[2 * self.z + near], self.keep_sem.at[half])
+
+    def first(self):
+        for half in range(2):
+            self.keep(half).start()
+        for link in (0, 1):
+            for half, _, _, near in self.sides():
+                self.start(None, half, 2 * self.z + near, 0, link, True)
+        self.enter(None, self.z, True)
+
+    def hop(self, d):
+        for side, onward in ((-1, 1), (1, 0)):
+            z = self.z + side * d
+            guard = z >= 0 if side < 0 else z < self.length
+            for half, _, _, near in self.sides():
+                self.arrive(guard, half, 2 * z + near, 0)
+                self.start(guard, half, 2 * z + near, 0, onward)
+            self.enter(guard, z)
+        self.crossing(d - 1)
+
+    def last(self):
+        self.crossing(self.length - 1)
+        if self.other is not None:
+            for half in range(2):
+                for at in range(2 * self.length):
+                    self.arrive(None, half, at, 1)
+        self.drain()
+        for half in range(2):
+            self.keep(half).wait()
 
     def crossing(self, d):
         if d == 0:
@@ -217,9 +221,10 @@
 
 
 class Reduce(Place):
-    def __init__(self, src, first, second, third, out, send, recv1, recv2, recv3, own=None, own_sem=None):
+    def __init__(self, kept, sent, got, first, second, third, out, send, recv1, recv2, recv3, own=None, own_sem=None):
         super().__init__()
-        self.src, self.first, self.second, self.third, self.out = src, first, second, third, out
+        self.kept, self.sent, self.got = kept, sent, got
+        self.first, self.second, self.third, self.out = first, second, third, out
         self.send, self.recv1, self.recv2, self.recv3 = send, recv1, recv2, recv3
         self.own, self.own_sem = own, own_sem
 
@@ -233,42 +238,42 @@
     def sides(self):
         return ((0, 3, 2, 1 - self.x, self.x), (1, 2, 3, 1 - self.y, self.y))
 
-    def kept(self, half, z, q):
-        return self.slot(z, q, self.y) if half == 0 else self.slot(z, self.x, q)
-
-    def sent(self, half, z, q):
-        return self.slot(z, q, 1 - self.y) if half == 0 else self.slot(z, 1 - self.x, q)
-
-    def load(self, half, z, q):
+    def loads(self, half, z, q):
         at = 2 * z + q
-        return pltpu.make_async_copy(
-            self.src.at[self.kept(half, z, q), half], self.own.at[half, at], self.own_sem.at[half, at]
-        )
+        copies = []
+        if self.own is not None:
+            copies.append(
+                pltpu.make_async_copy(self.kept(half, z, q), self.own.at[half, at], self.own_sem.at[half, at])
+            )
+        if self.got is not None:
+            copies.append(
+                pltpu.make_async_copy(self.got(half, z, q), self.first.at[half, at], self.recv1.at[half, at])
+            )
+        return copies
 
     def stage(self, k):
         z = self.target(k)
         for half, _, _, far, near in self.sides():
             for q in (far, near):
-                self.load(half, z, q).start()
+                for load in self.loads(half, z, q):
+                    load.start()
 
     def one(self, k):
         z = self.target(k)
         for half, link, _, far, near in self.sides():
             for q in (far, near):
                 self.post(
-                    None, self.src.at[self.sent(half, z, q), half], self.first.at[half, 2 * z + q],
+                    None, self.sent(half, z, q), self.first.at[half, 2 * z + q],
                     self.recv1.at[half, 2 * z + q], link,
                 )
 
     def join(self, half, z, q):
         at = 2 * z + q
-        self.receive(None, self.first.at[half, at], self.recv1.at[half, at])
-        if self.own is None:
-            mine = self.src.at[self.kept(half, z, q), half]
-        else:
-            self.load(half, z, q).wait()
-            mine = self.own.at[half, at]
-        accumulate(self.first.at[half, at], mine)
+        if self.got is None:
+            self.receive(None, self.first.at[half, at], self.recv1.at[half, at])
+        for load in self.loads(half, z, q):
+            load.wait()
+        accumulate(self.first.at[half, at], self.kept(half, z, q) if self.own is None else self.own.at[half, at])
 
     def two(self, k):
         z = self.target(k)
@@ -337,49 +342,75 @@
         pl.when(guard)(body)
 
 
-def spread_sems(chips, span):
-    length = chips // 2
+def spread_sems(length, rels):
     return [
-        pltpu.SemaphoreType.DMA((8 + (2 * length - 2) * 6 + (2 * length - 1) * 2 + 8,)),
-        pltpu.SemaphoreType.DMA((chips * span, 2)),
-        pltpu.SemaphoreType.DMA,
+        pltpu.SemaphoreType.DMA((4 + 2 * rels + (length - 1) * (8 + 4 * rels) + (2 * length - 1) * 2 + 8,)),
+        pltpu.SemaphoreType.DMA((2, rels, 2 * length)),
+        pltpu.SemaphoreType.DMA((2,)),
     ]
 
 
-def gather_small(src, wqkv_o, wout_o, par_o, dst, big, send, recv, own_sem, core_sem):
+def gather_small(src, wqkv_o, wout_o, par_o, own, other, own_s, other_s, big, send, recv, keep_sem, core_sem):
     core = lax.axis_index("core")
     sibling = {"core": 1 - core}
-    spread = Spread(src, dst.at[core], send, recv, own_sem)
+    halves = range(2)
+    spread = Spread(
+        [src.at[h] for h in halves], [own.at[h] for h in halves], [other.at[h] for h in halves], send, recv, keep_sem
+    )
     spread.greet(((None, sibling),))
-    for step in spread.steps():
-        step()
-    remote(dst.at[core], dst.at[core], core_sem.at[0], core_sem.at[1], sibling).start()
-    remote(dst.at[core], dst.at[core], core_sem.at[0], core_sem.at[1], sibling).wait_send()
-    remote(dst.at[1 - core], dst.at[1 - core], core_sem.at[0], core_sem.at[1], sibling).wait_recv()
-    width, span = wqkv_o.shape[0], spread.span
-    part, wide = width // (2 * spread.chips), width // span
-    for group in range(2 * spread.chips):
-        at = slice(part * group, part * (group + 1))
-        for t in range(span):
-            slot = (group // 2) * span + t
-            piece = jnp.concatenate([dst[group % 2, slot, 0], dst[group % 2, slot, 1]], -1).astype(F32)[:part]
-            for k in range(4):
-                big[at, width * k + wide * t : width * k + wide * (t + 1)] = piece[:, wide * k : wide * (k + 1)]
-            if t == 0:
-                big[at, 4 * width : 4 * width + 128] = piece[:, 4 * wide : 4 * wide + 128]
-    wqkv_o[...] = big[:, : 3 * width].astype(BF16)
-    wout_o[...] = big[:, 3 * width : 4 * width].astype(BF16)
-    par_o[...] = big[:, 4 * width : 4 * width + 128].T[0:8]
-
-
-def attention_forward(
-    tok, wqkv, wout, par, shard, normed_o, hidden_o, packed_o, mixed_o, lse_o, all_o, xs, send, recv, own_sem
-):
+    spread.first()
+    for d in range(1, spread.length):
+        spread.hop(d)
+    spread.last()
+    across = [remote(a, b, core_sem.at[0, i], core_sem.at[1, i], sibling)
+              for i, (a, b) in enumerate(((own, own_s), (other, other_s)))]
+    for copy in across:
+        copy.start()
+    width = wqkv_o.shape[0]
+    part, wide = width // (2 * spread.chips), width // spread.span
+
+    def place(core_of, parts, rel):
+        for z in range(spread.length):
+            for q in range(2):
+                for half in halves:
+                    piece = parts[half, 2 * z + q].astype(F32)[:part]
+                    x = q if half == 0 else (spread.x if rel == 0 else 1 - spread.x)
+                    t = q if half == 1 else (spread.y if rel == 0 else 1 - spread.y)
+                    group = (2 * z + x) * 2 + core_of
+                    at = pl.ds(pl.multiple_of(part * group, 8), part)
+                    big[half, t, at, :] = piece
+
+    place(core, own, 0)
+    place(core, other, 1)
+    for copy in across:
+        copy.wait()
+    place(1 - core, own_s, 0)
+    place(1 - core, other_s, 1)
+    pieces = [jnp.concatenate([big[0, t], big[1, t]], -1) for t in range(spread.span)]
+    for k in range(4):
+        line = jnp.concatenate([p[:, wide * k : wide * (k + 1)] for p in pieces], -1).astype(BF16)
+        if k < 3:
+            wqkv_o[:, width * k : width * (k + 1)] = line
+        else:
+            wout_o[...] = line
+    par_o[...] = pieces[0][:, 4 * wide : 4 * wide + 128].T[0:8]
+
+
+def attention_forward(custom, tok, wqkv, wout, par, *refs):
     rows, width = tok.shape
-    spread = Spread(shard, all_o, send, recv, own_sem)
-    spread.greet()
-    first, *rest = spread.steps()
-    first()
+    if custom:
+        (
+            shard, normed_o, hidden_o, packed_o, mixed_o, lse_o, normed_s, e0, e1, f0, f1, l0, l1,
+            xs, e_send, e_recv, e_keep, l_send, l_recv, l_keep, core_sem,
+        ) = refs
+        early = Spread([shard.at[0], shard.at[1]], [e0, e1], [f0, f1], e_send, e_recv, e_keep)
+        late = Spread([shard.at[2], shard.at[3]], [l0, l1], None, l_send, l_recv, l_keep)
+        sibling = {"core": 1 - lax.axis_index("core")}
+        early.greet(((None, sibling),))
+        early.first()
+        late.first()
+    else:
+        normed_o, hidden_o, packed_o, mixed_o, lse_o, xs = refs
     fill(xs, tok, rows)
     lane = lax.broadcasted_iota(jnp.int32, (1, 128), 1)
     low = lane < HEAD_DIM
@@ -421,36 +452,74 @@
         return carry
 
     images = rows // SEQ
-    lax.fori_loop(0, images // 2, image, 0)
-    rest[0]()
-    lax.fori_loop(images // 2, images, image, 0)
-    for step in rest[1:]:
-        step()
-
-
-def attention_backward(
-    custom, tok, cot, hidden_r, packed_r, mixed_r, lse_r, own, other, wqkv, wout, par, grads,
-    out_o, gtok_o, *refs,
-):
+    if not custom:
+        lax.fori_loop(0, images, image, 0)
+        return
+    lax.fori_loop(0, 6, image, 0)
+    early.hop(1)
+    late.hop(1)
+    lax.fori_loop(6, images, image, 0)
+    across = remote(normed_o, normed_s, core_sem.at[0], core_sem.at[1], sibling)
+    across.start()
+    for d in range(2, early.length):
+        early.hop(d)
+        late.hop(d)
+    early.last()
+    late.last()
+    across.wait()
+
+
+def attention_backward(custom, tok, cot, hidden_r, packed_r, mixed_r, lse_r, own, given, wqkv, wout, par, *refs):
+    rows, width = tok.shape
+    other = given
     if custom:
         (
-            gshard_o, small_o, xs, cs, outs, gtoks, gqkv_o, gout_o, gpar_o, pile, theirs,
-            w_own, w1, w2, w3, s1, s2, s3, w_send, w_r1, w_r2, w_r3, w_own_sem,
-            s_send, s_r1, s_r2, s_r3, core_sem,
+            ek0, ek1, er0, er1, lk0, lk1, ls0, ls1,
+            out_o, gtok_o, early_o, late_o, small_o, xs, cs, outs, gtoks, gqkv_o, gout_o, gpar_o, pile, theirs, others,
+            *room,
         ) = refs
         core = lax.axis_index("core")
         sibling = {"core": 1 - core}
-        big = Reduce(grads, w1, w2, w3, gshard_o, w_send, w_r1, w_r2, w_r3, w_own, w_own_sem)
-        little = Reduce(pile.at[core], s1, s2, s3, small_o, s_send, s_r1, s_r2, s_r3)
-        big.greet(((None, sibling),))
-        ranks = range(big.length)
-        big.one(0)
-        big.one(1)
+        (e_own, e1, e2, e3, l_own, l1, l2, l3, s1, s2, s3,
+         e_send, e_r1, e_r2, e_r3, e_sem, l_send, l_r1, l_r2, l_r3, l_sem, s_send, s_r1, s_r2, s_r3, core_sem) = room
+        ek, er, lk, ls = (ek0, ek1), (er0, er1), (lk0, lk1), (ls0, ls1)
+        early = Reduce(
+            lambda half, z, q: ek[half].at[2 * z + q], None, lambda half, z, q: er[half].at[2 * z + q],
+            e1, e2, e3, early_o, e_send, e_r1, e_r2, e_r3, e_own, e_sem,
+        )
+        late = Reduce(
+            lambda half, z, q: lk[half].at[2 * z + q], lambda half, z, q: ls[half].at[2 * z + q], None,
+            l1, l2, l3, late_o, l_send, l_r1, l_r2, l_r3, l_own, l_sem,
+        )
+        def pile_at(half, z, x, y):
+            return pile.at[core, late.slot(z, x, y), half]
+
+        little = Reduce(
+            lambda half, z, q: pile_at(half, z, q, late.y) if half == 0 else pile_at(half, z, late.x, q),
+            lambda half, z, q: pile_at(half, z, q, 1 - late.y) if half == 0 else pile_at(half, z, 1 - late.x, q),
+            None, s1, s2, s3, small_o, s_send, s_r1, s_r2, s_r3,
+        )
+        late.greet(((None, sibling),))
+        ranks = range(late.length)
+        middle = others.shape[0] // 2
+
+        def rows_across(i):
+            part = pl.ds(i * middle, middle)
+            return remote(given.at[part], others.at[part], core_sem.at[0, i], core_sem.at[1, i], sibling)
+
+        for i in range(2):
+            rows_across(i).start()
+        late.one(0)
         for k in ranks:
-            big.stage(k)
+            early.stage(k)
+            late.stage(k)
+        early.two(0)
+        late.one(1)
+        early.two(1)
+        other = others
+        rows_across(0).wait()
     else:
-        gqkv_o, gout_o, gpar_o, xs, cs, outs, gtoks = refs
-    rows, width = tok.shape
+        out_o, gtok_o, gqkv_o, gout_o, gpar_o, xs, cs, outs, gtoks = refs
     fill(xs, tok, rows)
     fill(cs, cot, rows)
     gqkv_o[...] = jnp.zeros_like(gqkv_o)
@@ -525,16 +594,23 @@
         return
 
     lax.fori_loop(0, 3, image, 0)
-    big.two(0)
-    big.one(2)
+    rows_across(1).wait()
+    late.two(0)
+    late.one(2)
+    early.two(2)
+    early.three(0)
     lax.fori_loop(3, 6, image, 0)
-    big.two(1)
-    big.one(3)
+    late.two(1)
+    late.one(3)
+    early.two(3)
+    early.three(1)
+    late.three(0)
     lax.fori_loop(6, 8, image, 0)
-    big.three(0)
+    late.two(2)
+    early.three(2)
     lax.fori_loop(8, images, image, 0)
-    span = big.span
-    part, wide = width // (2 * big.chips), width // span
+    span = late.span
+    part, wide = width // (2 * late.chips), width // span
     vectors = gpar_o[...].T
     for t in range(span):
         table = jnp.concatenate(
@@ -542,17 +618,19 @@
             + [gout_o[:, wide * t : wide * (t + 1)], vectors, jnp.zeros_like(vectors)],
             -1,
         )
-        for group in range(2 * big.chips):
+        for group in range(2 * late.chips):
             for half in range(2):
                 pile[group % 2, (group // 2) * span + t, half] = table[
                     part * group : part * (group + 1), 512 * half : 512 * (half + 1)
                 ]
+
     def across():
-        return remote(pile.at[1 - core], theirs, core_sem.at[0], core_sem.at[1], sibling)
+        return remote(pile.at[1 - core], theirs, core_sem.at[0, 2], core_sem.at[1, 2], sibling)
 
     across().start()
-    big.two(2)
-    big.three(1)
+    late.two(3)
+    late.three(1)
+    early.three(3)
     finish()
     across().wait()
 
@@ -564,14 +642,14 @@
     lax.fori_loop(0, theirs.shape[0], merge, 0)
     for k in ranks:
         little.one(k)
-    big.two(3)
-    big.three(2)
+    late.three(2)
     for k in ranks:
         little.two(k)
-    big.three(3)
+    late.three(3)
     for k in ranks:
         little.three(k)
-    big.drain()
+    early.drain()
+    late.drain()
     little.drain()
 
 
@@ -585,32 +663,42 @@
     return jnp.where(v < 0, q, 1.0 - q), e * INV_ROOT_TAU
 
 
-def experts(
-    cnt, rown, rsib, cown, csib, town, tsib, w_ref,
-    pown, psib, g_ref, xb, gb, tmpx, tmpg, acc1, acc2, off, dst, base, tot,
-):
+def experts(row, prior, cnt, rown, rsib, cown, csib, town, tsib, *refs):
+    if prior:
+        pown_i, psib_i, *refs = refs
+    else:
+        pown_i = psib_i = None
+    (
+        own0, oth0, own1, oth1, pown, psib, k0, n0, k1, n1,
+        xb, gb, tmpx, tmpg, acc1, acc2, wa, wb, fw, bk, off, dst, base, tot,
+    ) = refs
     number = pl.num_programs(0)
     e_now = pl.program_id(0)
     depth = town.shape[2]
     width = rown.shape[1]
-    slots = tmpx.shape[0]
-    step = slots // 3
 
     def blocks(fn):
-        for side, (table, r, c, out) in enumerate(((town, rown, cown, pown), (tsib, rsib, csib, psib))):
-            def body(j, carry, side=side, table=table, r=r, c=c, out=out):
-                fn(side * BLOCKS + j, table[j], r, c, out, pl.ds(pl.multiple_of(j * depth, ALIGN), depth))
+        for side, args in enumerate(((town, rown, cown, pown, pown_i), (tsib, rsib, csib, psib, psib_i))):
+            def body(j, carry, side=side, args=args):
+                fn(side * BLOCKS + j, args[0][j], *args[1:], pl.ds(pl.multiple_of(j * depth, ALIGN), depth))
                 return carry
 
             lax.fori_loop(0, BLOCKS, body, 0)
 
     def onehot(table, at):
-        slot = (lax.broadcasted_iota(jnp.int32, (step, 1), 0) + at).astype(F32)
-        first = table[0:1, :] == slot
-        second = table[1:2, :] == slot
+        slot = (lax.broadcasted_iota(jnp.int32, (STEP, 1), 0) + at).astype(F32)
+        first = table[row : row + 1, :] == slot
+        second = table[row + 1 : row + 2, :] == slot
         gate = jnp.where(first, table[2:3, :], jnp.where(second, table[3:4, :], 0.0))
         pick = jnp.where(first | second, 1.0, 0.0).astype(BF16)
         return pick, jnp.sum(gate, -1, keepdims=True)
+
+    def padded(k):
+        return (cnt[k] + (ALIGN - 1)) // ALIGN * ALIGN
+
+    def steps(b):
+        last = b * number + number - 1
+        return (off[last] + padded(last) + (STEP - 1)) // STEP
 
     def segments(b, move):
         def per(e, carry):
@@ -624,7 +712,7 @@
                 )
                 return carry
 
-            return lax.fori_loop(0, (cnt[k] + (ALIGN - 1)) // ALIGN, tile, carry)
+            return lax.fori_loop(0, padded(k) // ALIGN, tile, carry)
 
         lax.fori_loop(0, number, per, 0)
 
@@ -635,7 +723,7 @@
 
             def plan_block(b, run):
                 dst[b * number + e] = at + run
-                return run + (cnt[b * number + e] + (ALIGN - 1)) // ALIGN * ALIGN
+                return run + padded(b * number + e)
 
             total = lax.fori_loop(0, 2 * BLOCKS, plan_block, 0)
             tot[e] = total
@@ -646,19 +734,22 @@
         def plan_off(b, carry):
             def one(e, run):
                 off[b * number + e] = run
-                return run + (cnt[b * number + e] + (ALIGN - 1)) // ALIGN * ALIGN
+                return run + padded(b * number + e)
 
             lax.fori_loop(0, number, one, 0)
             return carry
 
         lax.fori_loop(0, 2 * BLOCKS, plan_off, 0)
 
-        def dispatch(b, table, r, c, out, here):
-            rows, cots = r[here, :], c[here, :]
-            for k in range(3):
-                pick, gate = onehot(table, k * step)
-                tmpx[k * step : (k + 1) * step, :] = nn(pick, rows).astype(BF16)
-                tmpg[k * step : (k + 1) * step, :] = (nn(pick, cots) * gate).astype(BF16)
+        def dispatch(b, table, r, c, out, before, here):
+            def some(k, carry):
+                at = pl.multiple_of(k * STEP, ALIGN)
+                pick, gate = onehot(table, at)
+                tmpx[pl.ds(at, STEP), :] = nn(pick, r[here, :]).astype(BF16)
+                tmpg[pl.ds(at, STEP), :] = (nn(pick, c[here, :]) * gate).astype(BF16)
+                return carry
+
+            lax.fori_loop(0, steps(b), some, 0)
 
             def move(local, far):
                 xb[far, :] = tmpx[local, :]
@@ -683,15 +774,24 @@
 
         lax.fori_loop(0, number, clear, 0)
 
-    shards, units = w_ref.shape[0], w_ref.shape[2] // 2
-    hidden = shards * units
+    shards, units = own0.shape[0], own0.shape[2] // 2
+    middle = shards * units
+    lower = e_now < number // 2
+
+    def load(own, other):
+        for i, ref in enumerate((own, other)):
+            to = slice(i * middle, (i + 1) * middle)
+            wa[to, :] = ref[:, 0, 0:units].reshape(middle, width)
+            wb[to, :] = ref[:, 0, units:].reshape(middle, width)
+
+    pl.when(lower)(lambda: load(own0, oth0))
+    pl.when(~lower)(lambda: load(own1, oth1))
     acc1[...] = jnp.zeros_like(acc1)
     acc2[...] = jnp.zeros_like(acc2)
 
     def chunk(t, carry):
         here = pl.ds(pl.multiple_of(base[e_now] + t * CHUNK, ALIGN), CHUNK)
-        first = w_ref[:, 0, 0:units].reshape(hidden, width)
-        second = w_ref[:, 0, units:].reshape(hidden, width)
+        first, second = wa[...], wb[...]
         x, g = xb[here, :], gb[here, :]
         v = nt(x, first)
         big, small = gelu_parts(v)
@@ -704,27 +804,97 @@
         return carry
 
     lax.fori_loop(0, (tot[e_now] + (CHUNK - 1)) // CHUNK, chunk, 0)
-    g_ref[:, 0, 0:units] = acc1[...].reshape(shards, units, width).astype(BF16)
-    g_ref[:, 0, units:] = acc2[...].reshape(shards, units, width).astype(BF16)
+
+    def save(kept, sent):
+        for i, ref in enumerate((kept, sent)):
+            part = slice(i * middle, (i + 1) * middle)
+            ref[:, 0, 0:units] = acc1[part, :].reshape(shards, units, width).astype(BF16)
+            ref[:, 0, units:] = acc2[part, :].reshape(shards, units, width).astype(BF16)
+
+    pl.when(lower)(lambda: save(k0, n0))
+    pl.when(~lower)(lambda: save(k1, n1))
 
     @pl.when(e_now == number - 1)
     def _():
-        def combine(b, table, r, c, out, here):
+        def combine(b, table, r, c, out, before, here):
             def move(local, far):
                 tmpx[local, :] = xb[far, :]
                 tmpg[local, :] = gb[far, :]
 
             segments(b, move)
-            forward, back = 0.0, 0.0
-            for k in range(3):
-                pick, gate = onehot(table, k * step)
-                part = slice(k * step, (k + 1) * step)
-                forward += tn(pick, (tmpx[part, :].astype(F32) * gate).astype(BF16))
-                back += tn(pick, tmpg[part, :])
-            out[here, 0:width] = forward.astype(BF16)
-            out[here, width:] = back.astype(BF16)
+            if before is None:
+                fw[...] = jnp.zeros_like(fw)
+                bk[...] = jnp.zeros_like(bk)
+            else:
+                fw[...] = before[here, 0:width].astype(F32)
+                bk[...] = before[here, width:].astype(F32)
+
+            def some(k, carry):
+                at = pl.multiple_of(k * STEP, ALIGN)
+                pick, gate = onehot(table, at)
+                fw[...] += tn(pick, (tmpx[pl.ds(at, STEP), :].astype(F32) * gate).astype(BF16))
+                bk[...] += tn(pick, tmpg[pl.ds(at, STEP), :])
+                return carry
+
+            lax.fori_loop(0, steps(b), some, 0)
+            out[here, 0:width] = fw[...].astype(BF16)
+            out[here, width:] = bk[...].astype(BF16)
 
         blocks(combine)
+
+
+def run_experts(late, tables, counts, row_refs, weights, prior):
+    padded, width = row_refs[0].shape
+    number, n_blocks = 2 * weights[0].shape[1], 2 * BLOCKS
+    depth = padded // BLOCKS
+    pairs = 4 * padded
+    room = -(-(pairs + n_blocks * number * (ALIGN - 1) + number * (CHUNK - ALIGN)) // CHUNK) * CHUNK
+    slots = -(-(2 * depth + number * (ALIGN - 1)) // STEP) * STEP
+    shards, _, lines, _ = weights[0].shape
+    held = shards * lines
+
+    def full(*shape):
+        return pl.BlockSpec(shape, lambda e, *_: (0,) * len(shape), pipeline_mode=pl.Buffered(1))
+
+    block = (shards, 1, lines, width)
+    lower = pl.BlockSpec(block, lambda e, *_: (0, jnp.minimum(e, number // 2 - 1), 0, 0))
+    upper = pl.BlockSpec(block, lambda e, *_: (0, jnp.maximum(e - number // 2, 0), 0, 0))
+    sums = full(padded, 2 * width)
+    grad = whole(weights[0].shape, BF16)
+    return pl.pallas_call(
+        functools.partial(experts, 5 if late else 0, prior is not None),
+        out_shape=(whole((padded, 2 * width), BF16),) * 2 + (grad,) * 4,
+        grid_spec=pltpu.PrefetchScalarGridSpec(
+            num_scalar_prefetch=1,
+            grid=(number,),
+            in_specs=[full(padded, width)] * 4
+            + [full(*tables[0].shape)] * 2
+            + [sums] * (0 if prior is None else 2)
+            + [lower, lower, upper, upper],
+            out_specs=(sums, sums, lower, lower, upper, upper),
+            scratch_shapes=[
+                pltpu.VMEM((room, width), BF16),
+                pltpu.VMEM((room, width), BF16),
+                pltpu.VMEM((slots, width), BF16),
+                pltpu.VMEM((slots, width), BF16),
+                pltpu.VMEM((held, width), F32),
+                pltpu.VMEM((held, width), F32),
+                pltpu.VMEM((held, width), BF16),
+                pltpu.VMEM((held, width), BF16),
+                pltpu.VMEM((depth, width), F32),
+                pltpu.VMEM((depth, width), F32),
+                pltpu.SMEM((n_blocks * number,), jnp.int32),
+                pltpu.SMEM((n_blocks * number,), jnp.int32),
+                pltpu.SMEM((number,), jnp.int32),
+                pltpu.SMEM((number,), jnp.int32),
+            ],
+        ),
+        compiler_params=pltpu.CompilerParams(
+            vmem_limit_bytes=VMEM_LIMIT, dimension_semantics=("arbitrary",)
+        ),
+        cost_estimate=pl.CostEstimate(flops=25 * 10**9, bytes_accessed=20 * 10**6, transcendentals=6 * 10**6),
+        name="experts_late" if late else "experts_early",
+    )(counts, *row_refs, *tables, *(() if prior is None else prior), *weights)
 
 
 def route(ids, gates, number, padded):
@@ -734,21 +904,26 @@
     gates = jnp.pad(gates, ((0, 0), (0, padded - rows)))
     ids = ids.reshape(2, BLOCKS, 1, depth)
     gates = gates.reshape(2, BLOCKS, 1, depth)
-    match = ids == jnp.arange(number, dtype=jnp.int32)[None, None, :, None]
+    listed = jnp.arange(number, dtype=jnp.int32)
+    match = ids == listed[None, None, :, None]
     named = (match[0] | match[1]).astype(BF16)
     order = jnp.arange(depth)
     earlier = (order[:, None] < order[None, :]).astype(BF16)
     rank = jnp.einsum("ber,rs->bes", named, earlier, preferred_element_type=F32)
     count = jnp.sum(named.astype(F32), -1)
     room = jnp.ceil(count * (1.0 / ALIGN)) * ALIGN
-    before = jnp.arange(number)
-    off = jnp.sum(jnp.where(before[None, :, None] < before[None, None, :], room[:, :, None], 0.0), 1)
+    middle = number // 2
+    ahead = (listed[:, None] < listed[None, :]) & (listed[:, None] // middle == listed[None, :] // middle)
+    off = jnp.sum(jnp.where(ahead[None], room[:, :, None], 0.0), 1)
     place = off[:, :, None] + rank
     slot = jnp.sum(jnp.where(match, place[None], 0.0), 2)
-    slot = jnp.where(ids[:, :, 0] >= 0, slot, -1.0)
-    table = jnp.stack([slot[0], slot[1], gates[0, :, 0], gates[1, :, 0]], 1)
+    flat = ids[:, :, 0]
+    first = jnp.where((flat >= 0) & (flat < middle), slot, -1.0)
+    second = jnp.where(flat >= middle, slot, -1.0)
     lanes = jnp.pad(count, ((0, 0), (0, depth - number)))
-    return jnp.concatenate([table, lanes[:, None, :], jnp.zeros((BLOCKS, 3, depth), F32)], 1)
+    return jnp.stack(
+        [first[0], first[1], gates[0, :, 0], gates[1, :, 0], lanes, second[0], second[1], jnp.zeros_like(lanes)], 1
+    )
 
 
 def whole(shape, dtype):
@@ -756,6 +931,7 @@
 
 
 IN_VMEM = pl.BlockSpec(memory_space=pltpu.VMEM)
+ANYWHERE = pl.BlockSpec(memory_space=pl.ANY)
 
 
 def on_device(
@@ -768,10 +944,9 @@
     groups, span = lax.axis_size(DP), lax.axis_size("tensor")
     part = width // groups
     wide = width // span
-    half = lax.axis_index("tensor")
-
+    side = lax.axis_index("tensor")
     chips = groups // 2
-    slots_all = chips * span
+    length = chips // 2
     custom = chips == 8 and span == 2 and part % 8 == 0
     vectors = jnp.stack([first_gain, first_shift, second_gain, second_shift], 1)
     small = jnp.concatenate(
@@ -783,7 +958,7 @@
         1,
     )
     shard = jnp.concatenate([expert_in.transpose(0, 2, 1), expert_out], 1)
-    shards, units = slots_all, shard.shape[1] // 2
+    units = shard.shape[1] // 2
     if custom:
         lines = -(-part // ALIGN) * ALIGN
         wqkv, wout, par = pl.pallas_call(
@@ -795,12 +970,10 @@
             ),
             in_specs=[IN_VMEM],
             out_specs=(IN_VMEM,) * 3,
-            scratch_shapes=[
-                pltpu.VMEM((2, slots_all, 2, lines, 512), BF16),
-                pltpu.VMEM((width, 4 * width + 128), F32),
-            ]
-            + spread_sems(chips, span)
-            + [pltpu.SemaphoreType.DMA((2,))],
+            scratch_shapes=[pltpu.VMEM((2, 2 * length, lines, 512), BF16)] * 4
+            + [pltpu.VMEM((2, span, width, 512), F32)]
+            + spread_sems(length, 2)
+            + [pltpu.SemaphoreType.DMA((2, 2))],
             compiler_params=pltpu.CompilerParams(collective_id=0, has_side_effects=True, vmem_limit_bytes=VMEM_LIMIT),
             name="gather_small",
         )(jnp.pad(small, ((0, lines - part), (0, 0))).reshape(lines, 2, 512).transpose(1, 0, 2))
@@ -811,85 +984,73 @@
         wqkv, wout = taken[:, :3].reshape(width, 3 * width), taken[:, 3]
         par = gathered[:, 0, :, 4 * wide : 4 * wide + 8].reshape(width, 8).T.astype(F32)
 
-    ids = lax.dynamic_slice_in_dim(expert_ids.T, half * rows, rows, 1)
-    gates = lax.dynamic_slice_in_dim(gate_weights.T, half * rows, rows, 1)
+    ids = lax.dynamic_slice_in_dim(expert_ids.T, side * rows, rows, 1)
+    gates = lax.dynamic_slice_in_dim(gate_weights.T, side * rows, rows, 1)
     table = route(ids, gates, number, padded)
     table_sib = lax.ppermute(table, "core", SWAP)
     cot_own = jnp.pad(cotangent, ((0, padded - rows), (0, 0)))
     cot_sib = lax.ppermute(cot_own, "core", SWAP)
 
-    normed, hidden, packed, mixed, lse, weights = pl.pallas_call(
-        attention_forward,
-        out_shape=(
-            whole((padded, width), BF16),
-            whole((padded, width), F32),
-            whole((padded, 3 * width), BF16),
-            whole((padded, width), BF16),
-            whole((padded, 128), F32),
-            whole((shards, 2, number // 2, 2 * units, width), BF16),
-        ),
-        in_specs=[IN_VMEM] * 5,
-        out_specs=(IN_VMEM,) * 5 + (pl.BlockSpec(memory_space=pl.ANY),),
-        scratch_shapes=[pltpu.VMEM((padded, width), BF16)] + spread_sems(chips, span),
-        compiler_params=pltpu.CompilerParams(vmem_limit_bytes=VMEM_LIMIT, collective_id=1, has_side_effects=True),
-        cost_estimate=pl.CostEstimate(flops=6 * 10**9, bytes_accessed=14 * 10**6, transcendentals=3 * 10**6),
-        name="attention_forward",
-    )(tokens, wqkv, wout, par, shard.reshape(2, number // 2, 2 * units, width))
-    weights = weights.reshape(shards, number, 2 * units, width)
-    regroup = units % ALIGN != 0
-    if regroup:
-        weights = weights.reshape(shards, number, 2, units, width)
-        weights = weights.transpose(1, 2, 0, 3, 4).reshape(1, number, 2 * shards * units, width)
-    normed_sib = lax.ppermute(normed, "core", SWAP)
-
-    counts = jnp.concatenate([table[:, 4, :number], table_sib[:, 4, :number]], 0).astype(jnp.int32).reshape(-1)
-    n_blocks = 2 * BLOCKS
-    room = -(-(4 * rows + n_blocks * number * (ALIGN - 1) + number * (CHUNK - ALIGN)) // CHUNK) * CHUNK
-    depth = padded // BLOCKS
-    slots = -(-(2 * depth + number * (ALIGN - 1)) // (3 * ALIGN)) * (3 * ALIGN)
-    held = weights.shape[0] * weights.shape[2] // 2
-
-    def full(*shape):
-        return pl.BlockSpec(shape, lambda e, *_: (0,) * len(shape), pipeline_mode=pl.Buffered(1))
-
-    by_expert = pl.BlockSpec(
-        (weights.shape[0], 1, weights.shape[2], width), lambda e, *_: (0, e, 0, 0)
+    row_shapes = (
+        whole((padded, width), BF16),
+        whole((padded, width), F32),
+        whole((padded, 3 * width), BF16),
+        whole((padded, width), BF16),
+        whole((padded, 128), F32),
     )
-    part_own, part_sib, grads = pl.pallas_call(
-        experts,
-        out_shape=(
-            whole((padded, 2 * width), BF16),
-            whole((padded, 2 * width), BF16),
-            whole(weights.shape, BF16),
-        ),
-        grid_spec=pltpu.PrefetchScalarGridSpec(
-            num_scalar_prefetch=1,
-            grid=(number,),
-            in_specs=[full(padded, width)] * 4 + [full(*table.shape)] * 2 + [by_expert],
-            out_specs=(full(padded, 2 * width), full(padded, 2 * width), by_expert),
-            scratch_shapes=[
-                pltpu.VMEM((room, width), BF16),
-                pltpu.VMEM((room, width), BF16),
-                pltpu.VMEM((slots, width), BF16),
-                pltpu.VMEM((slots, width), BF16),
-                pltpu.VMEM((held, width), F32),
-                pltpu.VMEM((held, width), F32),
-                pltpu.SMEM((n_blocks * number,), jnp.int32),
-                pltpu.SMEM((n_blocks * number,), jnp.int32),
-                pltpu.SMEM((number,), jnp.int32),
-                pltpu.SMEM((number,), jnp.int32),
-            ],
-        ),
-        compiler_params=pltpu.CompilerParams(
-            vmem_limit_bytes=VMEM_LIMIT, dimension_semantics=("arbitrary",)
-        ),
-        cost_estimate=pl.CostEstimate(flops=50 * 10**9, bytes_accessed=40 * 10**6, transcendentals=12 * 10**6),
-        name="experts",
-    )(counts, normed, normed_sib, cot_own, cot_sib, table, table_sib, weights)
-    part_other = lax.ppermute(part_sib, "core", SWAP)
-    if regroup:
-        grads = grads.reshape(number, 2, shards, units, width).transpose(2, 0, 1, 3, 4)
-        grads = grads.reshape(shards, number, 2 * units, width)
+    estimate = pl.CostEstimate(flops=6 * 10**9, bytes_accessed=14 * 10**6, transcendentals=3 * 10**6)
+    xs_scratch = [pltpu.VMEM((padded, width), BF16)]
+    quarter = number // 4
+    if custom:
+        held = whole((2 * length, quarter, 2 * units, width), BF16)
+        normed, hidden, packed, mixed, lse, normed_sib, e0, e1, f0, f1, l0, l1 = pl.pallas_call(
+            functools.partial(attention_forward, True),
+            out_shape=row_shapes + (row_shapes[0],) + (held,) * 6,
+            in_specs=[IN_VMEM] * 5,
+            out_specs=(IN_VMEM,) * 6 + (ANYWHERE,) * 6,
+            scratch_shapes=xs_scratch
+            + spread_sems(length, 2)
+            + spread_sems(length, 1)
+            + [pltpu.SemaphoreType.DMA((2,))],
+            compiler_params=pltpu.CompilerParams(vmem_limit_bytes=VMEM_LIMIT, collective_id=1, has_side_effects=True),
+            cost_estimate=estimate,
+            name="attention_forward",
+        )(tokens, wqkv, wout, par, shard.reshape(4, quarter, 2 * units, width))
+        across_y = functools.partial(lax.ppermute, axis_name="tensor", perm=SWAP)
+        across_x = functools.partial(lax.ppermute, axis_name="chip", perm=[(c, c ^ 1) for c in range(chips)])
+        early_weights = (e0, f0, e1, f1)
+        late_weights = (l0, across_y(l0), l1, across_x(l1))
+    else:
+        normed, hidden, packed, mixed, lse = pl.pallas_call(
+            functools.partial(attention_forward, False),
+            out_shape=row_shapes,
+            in_specs=[IN_VMEM] * 4,
+            out_specs=(IN_VMEM,) * 5,
+            scratch_shapes=xs_scratch,
+            compiler_params=pltpu.CompilerParams(vmem_limit_bytes=VMEM_LIMIT),
+            cost_estimate=estimate,
+            name="attention_forward",
+        )(tokens, wqkv, wout, par)
+        normed_sib = lax.ppermute(normed, "core", SWAP)
+        weights = lax.all_gather(shard, RING, axis=0, tiled=False)
+        shards = weights.shape[0]
+        weights = weights.reshape(2, shards // 2, 4, quarter, 2, units, width).transpose(2, 0, 3, 4, 1, 5, 6)
+        weights = weights.reshape(4, 2, 1, quarter, shards * units, width)
+        early_weights = tuple(weights[i, j] for i in (0, 1) for j in (0, 1))
+        late_weights = tuple(weights[i, j] for i in (2, 3) for j in (0, 1))
+
+    middle = number // 2
+    both_counts = jnp.concatenate([table[:, 4, :number], table_sib[:, 4, :number]], 0).astype(jnp.int32)
+    row_refs = (normed, normed_sib, cot_own, cot_sib)
+    tables = (table, table_sib)
+    own1, sib1, *early = run_experts(
+        False, tables, both_counts[:, :middle].reshape(-1), row_refs, early_weights, None
+    )
+    if custom:
+        got = (across_y(early[1]), across_x(early[3]))
+    part_own, part_sib, *late = run_experts(
+        True, tables, both_counts[:, middle:].reshape(-1), row_refs, late_weights, (own1, sib1)
+    )
 
     sums = [
         pltpu.VMEM((width, 3 * width), F32),
@@ -902,46 +1063,47 @@
         pltpu.VMEM((padded, width), BF16),
         pltpu.VMEM((padded, width), F32),
     ]
-    operands = (tokens, cotangent, hidden, packed, mixed, lse, part_own, part_other, wqkv, wout, par)
+    saved = (tokens, cotangent, hidden, packed, mixed, lse, part_own)
     shapes = (whole((rows, width), BF16), whole((rows, width), F32))
     estimate = pl.CostEstimate(flops=15 * 10**9, bytes_accessed=25 * 10**6, transcendentals=3 * 10**6)
     if custom:
-        length = chips // 2
-        block, tile = (number // 2, 2 * units, width), (part, 512)
-        output, grad_tokens, grad_shard, mine = pl.pallas_call(
+        block, tile = (quarter, 2 * units, width), (part, 512)
+        output, grad_tokens, early_grad, late_grad, mine = pl.pallas_call(
             functools.partial(attention_backward, True),
-            out_shape=shapes + (whole((2,) + block, F32), whole((2,) + tile, F32)),
-            in_specs=[IN_VMEM] * 11 + [pl.BlockSpec(memory_space=pl.ANY)],
-            out_specs=(IN_VMEM,) * 4,
+            out_shape=shapes + (whole((2,) + block, F32),) * 2 + (whole((2,) + tile, F32),),
+            in_specs=[IN_VMEM] * 7 + [ANYWHERE] + [IN_VMEM] * 3 + [ANYWHERE] * 8,
+            out_specs=(IN_VMEM,) * 5,
             scratch_shapes=rows_scratch
             + sums
-            + [pltpu.VMEM((2, shards, 2) + tile, F32), pltpu.VMEM((shards, 2) + tile, F32)]
-            + [pltpu.VMEM((2, 2 * length) + block, BF16)]
-            + reduce_room(length, block, BF16)
+            + [pltpu.VMEM((2, 2 * chips, 2) + tile, F32), pltpu.VMEM((2 * chips, 2) + tile, F32)]
+            + [pltpu.VMEM((padded, 2 * width), BF16)]
+            + ([pltpu.VMEM((2, 2 * length) + block, BF16)] + reduce_room(length, block, BF16)) * 2
             + reduce_room(length, tile, F32)
+            + (reduce_sems(length) + [pltpu.SemaphoreType.DMA((2, 2 * length))]) * 2
             + reduce_sems(length)
-            + [pltpu.SemaphoreType.DMA((2, 2 * length))]
-            + reduce_sems(length)
-            + [pltpu.SemaphoreType.DMA((2,))],
+            + [pltpu.SemaphoreType.DMA((2, 3))],
             compiler_params=pltpu.CompilerParams(
                 vmem_limit_bytes=VMEM_LIMIT, collective_id=2, has_side_effects=True
             ),
             cost_estimate=estimate,
             name="attention_backward",
-        )(*operands, grads.reshape((shards, 2) + block))
+        )(*saved, part_sib, wqkv, wout, par, early[0], early[2], *got, late[0], late[2], late[1], late[3])
         mine = mine.transpose(1, 0, 2).reshape(part, 1024)
-        grad_shard = grad_shard.reshape(number, 2 * units, width)
+        grad_shard = jnp.concatenate([early_grad, late_grad], 0).reshape(number, 2 * units, width)
     else:
+        part_other = lax.ppermute(part_sib, "core", SWAP)
         output, grad_tokens, gqkv, gout, gpar = pl.pallas_call(
             functools.partial(attention_backward, False),
             out_shape=shapes + tuple(whole(ref.shape, F32) for ref in sums),
-            in_specs=[IN_VMEM] * 11 + [pl.BlockSpec(memory_space=pl.ANY)],
+            in_specs=[IN_VMEM] * 11,
             out_specs=(IN_VMEM,) * 5,
             scratch_shapes=rows_scratch,
             compiler_params=pltpu.CompilerParams(vmem_limit_bytes=VMEM_LIMIT),
             cost_estimate=estimate,
             name="attention_backward",
-        )(*operands, grads)
+        )(*saved, part_other, wqkv, wout, par)
+        grads = jnp.stack(early + late).reshape(4, 2, quarter, 2, shards // 2, units, width)
+        grads = grads.transpose(1, 4, 0, 2, 3, 5, 6).reshape(shards, number, 2 * units, width)
         grad_shard = lax.psum_scatter(grads, RING, scatter_dimension=0, tiled=False).astype(F32)
         owed = jnp.concatenate([gqkv.reshape(width, 3, width), gout[:, None]], 1)
         owed = owed.reshape(groups, part, 4, span, wide).transpose(0, 3, 1, 2, 4)

time: 372 us -> 364 us (0.978); the launches traced: 373 us -> 360 us
  Pallas kernels: 346 us -> 335 us
  waiting for transfers between devices: 7.46 us -> 0.02 us
    pallas_call x1, Pallas kernels: 113 us -> 92.5 us  [on_device(): pl.pallas_call(functools.partial(attention_backward, True), out_shape=sha...]
    pallas_call x2 -> x3, Pallas kernels: 207 us -> 216 us  [the longest x2 153 us: run_experts(): pl.pallas_call(functools.partial(experts, 5 if late else 0, prior is not...]
    ppermute x2 -> x4, waiting for transfers between devices: 5.59 us -> 0.01 us  [the longest x2 0.01 us: on_device(): got = (across_y(early[1]), across_x(early[3]))]
    ppermute x2 -> x4, starting transfers between devices: 0.21 us -> 4.24 us  [the longest x2 2.15 us: on_device(): got = (across_y(early[1]), across_x(early[3]))]
    unnamed x38 -> x42, local copies, waits for them, and re-layouts: 7.46 us -> 7.89 us
  transfers between devices with their start and end apart: 4 -> 6, of which waited for: 2 -> 0; matrix products, arithmetic and copies ran while one was open for 1% -> 1% of each run, Pallas kernels for 30% -> 67%
where the time goes in v1:
time: 364 us; the launch traced here: 360 us
  Pallas kernels  335 us (92%)
  local copies, waits for them, and re-layouts  15.7 us (4%)
  starting transfers between devices  4.89 us (1%)
    pallas_call x2, Pallas kernels, run_experts(): pl.pallas_call(functools.partial(experts, 5 if late else 0, prior is not...  153 us
    pallas_call x1, Pallas kernels, on_device(): pl.pallas_call(functools.partial(attention_backward, True), out_shape=sha...  92.5 us
    pallas_call x1, Pallas kernels, on_device(): pl.pallas_call(functools.partial(attention_forward, True), out_shape=row_...  63.9 us
    pallas_call x1, Pallas kernels, on_device(): pl.pallas_call(gather_small, out_shape=(whole((width, 3 * width), BF16),...  25.8 us
    unnamed x42, local copies, waits for them, and re-layouts  7.89 us
  transfers between devices with their start and end apart: 6, of which 0 were waited for; matrix products, arithmetic and copies ran while one was open for 1% of the time, Pallas kernels for 67%

profile of v1, /device:TPU:0, one launch (start us, length us, event | category | flops | bytes accessed | tf_op | source)
XLA Modules:
  0.0 359.7 jit_solution(8931810478041685067)
XLA Ops:
  0.6 0.0 copy-start
  0.7 1.6 pad.29.cown
  2.3 0.0 copy-start.5
  2.3 0.0 copy-start.6
  2.4 0.6 collective-permute-start.1
  2.9 0.1 fusion.7
  3.0 0.1 dynamic-slice_bitcast_fusion.1
  3.1 0.1 eq.32
  3.2 0.1 convert_reduce_fusion
  3.3 0.1 select_reduce_fusion.1
  3.4 0.2 convolution_add_fusion
  3.6 0.1 select_reduce_fusion
  3.7 0.1 dynamic-slice_bitcast_fusion
  3.9 0.1 stack_squeeze.21
  4.0 0.1 stack_squeeze.20
  4.1 0.1 stack.27.town
  4.2 0.1 collective-permute-start
  4.4 0.1 copy.46
  4.5 0.1 reshape.173
  4.6 0.1 fusion.4
  4.7 0.6 copy.62
  5.3 25.8 %gather_small.1 = (bf16[384,1152]{1,0:T(8,128)(2,1)}, bf16[384,384]{1,0:T(8,128)(2,1)}, f32[8,384]{1,0:T(8,128)}) custom-call(bf16[2,32,512]{2,1,0:T(8,128)(2,1)} %bitcast.51), custom_call_target="tpu_custom_call" | custom-call | tf_op jit(solution)/shard_map/gather_small/pallas_call | solution.py:964
  31.2 0.9 pad_maximum_fusion.1
  32.0 63.9 %attention_forward.1 = (bf16[1984,384]{1,0:T(8,128)(2,1)}, f32[1984,384]{1,0:T(8,128)}, bf16[1984,1152]{1,0:T(8,128)(2,1)}, bf16[1984,384]{1,0:T(8,128)(2,1)}, f...) custom-call(bf16[1970,384]{1,0:T(8,128)(2,1)} %tok.3, ...), custom_call_target="tpu_custom_call" | custom-call | flops 6000000000 | bytes 14000000 | tf_op jit(solution)/shard_map/attention_forward/pallas_call | solution.py:1006
  96.0 1.0 collective-permute-start.2
  97.0 1.1 collective-permute-start.3
  98.1 0.1 fusion.10
  98.2 0.6 reshape.177.cnt
  98.8 0.6 reshape.176.cnt
  99.4 73.2 %experts_early.1 = (bf16[1984,768]{1,0:T(8,128)(2,1)}, bf16[1984,768]{1,0:T(8,128)(2,1)}, bf16[8,2,96,384]{3,2,1,0:T(8,128)(2,1)}, bf16[8,2,96,384]{3,2,1,0:T(8,...) custom-call(s32[32]{0:T(128)} %reshape.177.cnt, bf16[1984,384]{1,0:T(8,128)(2,1)} %get-tuple-element.49.rown, ...), custom_call_target="tpu_custom_call" | custom-call | flops 24999999488 | bytes 20000000 | tf_op jit(solution)/shard_map/experts_early/pallas_call | solution.py:864
  172.6 1.0 collective-permute-start.4
  173.6 1.1 collective-permute-start.5
  174.8 1.0 copy-done.16
  175.8 79.3 %experts_late.1 = (bf16[1984,768]{1,0:T(8,128)(2,1)}, bf16[1984,768]{1,0:T(8,128)(2,1)}, bf16[8,2,96,384]{3,2,1,0:T(8,128)(2,1)}, bf16[8,2,96,384]{3,2,1,0:T(8,1...) custom-call(s32[32]{0:T(128)} %reshape.176.cnt, bf16[1984,384]{1,0:T(8,128)(2,1)} %get-tuple-element.49.rown, ...), custom_call_target="tpu_custom_call" | custom-call | flops 24999999488 | bytes 20000000 | tf_op jit(solution)/shard_map/experts_late/pallas_call | solution.py:864
  255.2 1.0 copy-done.17
  256.2 0.4 copy-done.18
  256.6 92.5 %attention_backward.1 = (bf16[1970,384]{1,0:T(8,128)(2,1)}, f32[1970,384]{1,0:T(8,128)}, f32[2,2,96,384]{3,2,1,0:T(8,128)}, f32[2,2,96,384]{3,2,1,0:T(8,128)}, f32[2,24,512]{2,1,0:T(8,128)}) custom-call(bf16[1970,384]{1,0:T(8,128)(2,1)} %tok.3, bf16[1970,384]{1,0:T(8,128)(2,1)} %cot.1, f32[1984,384]{1,0:T(8,128)} %get-tuple-element.45.hidden_r, ...), custom_call_target="tpu_custom_call" | custom-call | flops 15000000512 | bytes 25000000 | tf_op jit(solution)/shard_map/attention_backward/pallas_call | solution.py:1071
  349.0 0.9 copy.56
  349.9 0.7 slice_reduce_fusion
  350.7 0.7 slice_bitcast_fusion.1
  351.4 0.1 reshape.179
  351.5 0.6 copy.54
  352.1 1.3 pad_maximum_fusion
  353.5 1.1 fusion.9
  354.6 0.7 copy-done.4
  355.3 1.1 copy.65
  356.4 1.3 copy-done.2
  357.7 1.6 copy.66
  (53 shorter events, 0.3 us)
Async XLA Ops:
  0.6 2.4 copy-start
  0.7 3.1 copy-start.10
  0.7 3.7 %copy-start.11 = (bf16[24]{0:T(256)(128)(2,1)S(1)}, bf16[24]{0:T(256)(128)(2,1)}, u32[]{:S(2)}) copy-start(bf16[24]{0:T(256)(128)(2,1)} %param.18) | copy-start | bytes 148
  0.7 3.7 %copy-start.12 = (bf16[24]{0:T(256)(128)(2,1)S(1)}, bf16[24]{0:T(256)(128)(2,1)}, u32[]{:S(2)}) copy-start(bf16[24]{0:T(256)(128)(2,1)} %param.17) | copy-start | bytes 148
  0.7 3.6 %copy-start.13 = (bf16[24]{0:T(256)(128)(2,1)S(1)}, bf16[24]{0:T(256)(128)(2,1)}, u32[]{:S(2)}) copy-start(bf16[24]{0:T(256)(128)(2,1)} %param.16) | copy-start | bytes 148
  0.7 3.6 %copy-start.14 = (bf16[24]{0:T(256)(128)(2,1)S(1)}, bf16[24]{0:T(256)(128)(2,1)}, u32[]{:S(2)}) copy-start(bf16[24]{0:T(256)(128)(2,1)} %param.15) | copy-start | bytes 148
  0.7 3.8 %copy-start.8 = (bf16[24,3,192]{2,0,1:T(8,128)(2,1)S(1)}, bf16[24,3,192]{2,0,1:T(8,128)(2,1)}, u32[]{:S(2)}) copy-start(bf16[24,3,192]{2,0,1:T(8,128)(2,1)} %param.13) | copy-start | bytes 82948
  2.3 29.7 %copy-start.3 = (bf16[1984,384]{1,0:T(8,128)(2,1)}, bf16[1984,384]{1,0:T(8,128)(2,1)S(1)}, u32[]{:S(2)}) copy-start(bf16[1984,384]{1,0:T(8,128)(2,1)S(1)} %pad.29.cown) | copy-start | bytes 4571140
  2.3 2.3 copy-start.9
  2.3 28.8 %copy-start.5 = (bf16[8,48,384]{2,1,0:T(8,128)(2,1)S(1)}, bf16[8,48,384]{2,1,0:T(8,128)(2,1)}, u32[]{:S(2)}) copy-start(bf16[8,48,384]{2,1,0:T(8,128)(2,1)} %param.20) | copy-start | bytes 884740
  2.3 28.8 %copy-start.6 = (bf16[8,384,48]{1,2,0:T(8,128)(2,1)S(1)}, bf16[8,384,48]{1,2,0:T(8,128)(2,1)}, u32[]{:S(2)}) copy-start(bf16[8,384,48]{1,2,0:T(8,128)(2,1)} %param.19) | copy-start | bytes 884740
  2.4 97.0 %collective-permute-start.1 = (bf16[1984,384]{1,0:T(8,128)(2,1)S(1)}, bf16[1984,384]{1,0:T(8,128)(2,1)}, u32[]{:S(2)}, u32[]{:S(2)}) collective-permute-start(bf16[1984,384]{1,0:T(8,128)(2,1)S(1)} %pad.29.cown), channel_id=1, source_target_pairs={{0,2},{2,0},{1,3},{3,1},{4,6},{6,4},{5,7},{7,5},{8,10},{10,8},{9,1... | collective-permute-start | bytes 4571144 | tf_op jit(solution)/shard_map/ppermute | solution.py:992
  4.2 91.8 %copy-start.7 = (f32[4,8,496]{2,1,0:T(8,128)}, f32[4,8,496]{2,1,0:T(8,128)S(1)}, u32[]{:S(2)}) copy-start(f32[4,8,496]{2,1,0:T(8,128)S(1)} %stack.27.town) | copy-start | bytes 190468
  4.2 93.8 %collective-permute-start = (f32[4,8,496]{2,1,0:T(8,128)S(1)}, f32[4,8,496]{2,1,0:T(8,128)S(1)}, u32[]{:S(2)}, u32[]{:S(2)}) collective-permute-start(f32[4,8,496]{2,1,0:T(8,128)S(1)} %stack.27.town), channel_id=1, source_target_pairs={{0,2},{2,0},{1,3},{3,1},{4,6},{6,4},{5,7},{7,5},{8,10},{10,8},{9,1... | collective-permute-start | bytes 190472 | tf_op jit(solution)/shard_map/ppermute | solution.py:990
  96.0 78.8 %collective-permute-start.2 = (bf16[8,2,96,384]{3,2,1,0:T(8,128)(2,1)}, bf16[8,2,96,384]{3,2,1,0:T(8,128)(2,1)S(1)}, u32[]{:S(2)}, u32[]{:S(2)}) collective-permute-start(bf16[8,2,96,384]{3,2,1,0:T(8,128)(2,1)} %get-tuple-element.57.refs_2_), channel_id=1, source_target_pairs={{0,1},{1,0},{2,3},{3,2},{4,5},{5,4},{6,7},{7,6},{8,9},{9,8},{10,11... | collective-permute-start | bytes 3538952 | tf_op jit(solution)/shard_map/ppermute | solution.py:1022
  97.0 77.8 %collective-permute-start.3 = (bf16[8,2,96,384]{3,2,1,0:T(8,128)(2,1)}, bf16[8,2,96,384]{3,2,1,0:T(8,128)(2,1)}, u32[]{:S(2)}, u32[]{:S(2)}) collective-permute-start(bf16[8,2,96,384]{3,2,1,0:T(8,128)(2,1)} %get-tuple-element.58.refs_4_), channel_id=1, source_target_pairs={{0,4},{4,0},{8,12},{12,8},{16,20},{20,16},{24,28},{28,24},{1,5},{5... | collective-permute-start | bytes 3538952 | tf_op jit(solution)/shard_map/ppermute | solution.py:1022
  98.1 1.3 copy-start.15
  172.6 82.5 %collective-permute-start.4 = (bf16[8,2,96,384]{3,2,1,0:T(8,128)(2,1)}, bf16[8,2,96,384]{3,2,1,0:T(8,128)(2,1)S(1)}, u32[]{:S(2)}, u32[]{:S(2)}) collective-permute-start(bf16[8,2,96,384]{3,2,1,0:T(8,128)(2,1)} %get-tuple-element.63), channel_id=1, source_target_pairs={{0,1},{1,0},{2,3},{3,2},{4,5},{5,4},{6,7},{7,6},{8,9},{9,8},{10,11... | collective-permute-start | bytes 3538952 | tf_op jit(solution)/shard_map/ppermute | solution.py:1050
  173.6 81.5 %collective-permute-start.5 = (bf16[8,2,96,384]{3,2,1,0:T(8,128)(2,1)}, bf16[8,2,96,384]{3,2,1,0:T(8,128)(2,1)S(1)}, u32[]{:S(2)}, u32[]{:S(2)}) collective-permute-start(bf16[8,2,96,384]{3,2,1,0:T(8,128)(2,1)} %get-tuple-element.64), channel_id=1, source_target_pairs={{0,4},{4,0},{8,12},{12,8},{16,20},{20,16},{24,28},{28,24},{1,5},{5... | collective-permute-start | bytes 3538952 | tf_op jit(solution)/shard_map/ppermute | solution.py:1050
  174.8 1.0 copy-start.16
  255.1 1.0 copy-start.17
  255.2 1.4 copy-start.18
  353.5 1.8 copy-start.4
  355.3 2.4 copy-start.2
  357.7 1.6 copy-start.1
